TPU v7x, 32 devices: a whole 2x2x4 slice. The times are simulated.
32 devices in a mesh: dp: 4 (over x, y), tp: 8 (over z, core).
Axes of the slice: x: 2, y: 2, z: 4, core: 2. Of those that a mesh axis runs over, the one named last changes fastest.
Arguments:
- hidden: bfloat16 [256, 4, 1536], P('dp'), parts along dimension 0
- norm_gain: float32 [1536], replicated
- w_head: bfloat16 [1536, 151936], P(None, 'tp')
- draft_probs: float32 [256, 3, 151936], P('dp', None, 'tp'), parts along dimension 0
- draft_tokens: int32 [256, 3], P('dp'), parts along dimension 0
- temperature: float32 [256], P('dp'), parts along dimension 0
Outputs:
- output 1: float32 [256, 3], P('dp'), parts along dimension 0
- output 2: float32 [256, 3], P('dp'), parts along dimension 0
- output 3: float32 [256, 3, 151936], P('dp', None, 'tp'), parts along dimension 0
- output 4: float32 [256], P('dp'), parts along dimension 0
There are 4 independent parts. A program takes and returns all parts, laid end to end along the dimension named above; an argument that names none is the same for every part.
All inputs are finite; a program needn't handle non-finite values.
Results may differ from a plain program's by a relative error of at most 0.001.
Values sent between devices are 32-bit elements.
A program may use at most 1 GiB of HBM per device.

v0:
```python
import jax
import jax.numpy as jnp
from jax import lax
from jax.sharding import PartitionSpec as P


def solution(mesh):
    def local_step(hidden, norm_gain, w_head, draft_probs, draft_tokens, value_a11):
        draft_len = draft_probs.shape[1]
        shard_vocab = w_head.shape[1]
        hidden_f32 = hidden.astype(jnp.float32)
        inv_rms = lax.rsqrt(jnp.mean(hidden_f32 * hidden_f32, axis=-1, keepdims=True) + 1e-5)
        normed = (hidden_f32 * inv_rms * norm_gain).astype(jnp.bfloat16)
        logits = jnp.einsum('cle,ew->clw', normed, w_head, preferred_element_type=jnp.float32)
        scaled = logits / value_a11[:, None, None]
        row_max = lax.pmax(jnp.max(scaled, axis=-1), 'tp')
        local_sum = jnp.sum(jnp.exp(scaled - row_max[:, :, None]), axis=-1)
        local_idx = draft_tokens - lax.axis_index('tp') * shard_vocab
        is_owned = (local_idx >= 0) & (local_idx < shard_vocab)
        safe_idx = jnp.clip(local_idx, 0, shard_vocab - 1)[:, :, None]
        tok_scaled = jnp.where(is_owned, jnp.take_along_axis(scaled[:, :draft_len], safe_idx, axis=-1)[:, :, 0], 0.0)
        tok_draft = jnp.where(is_owned, jnp.take_along_axis(draft_probs, safe_idx, axis=-1)[:, :, 0], 0.0)
        total_sum, tok_scaled, tok_draft = lax.psum((local_sum, tok_scaled, tok_draft), 'tp')
        row_lse = row_max + jnp.log(total_sum)
        draft_lse = row_lse[:, :draft_len]
        tok_target = jnp.exp(tok_scaled - draft_lse)
        accept = jnp.minimum(1.0, tok_target / tok_draft)
        excess = jnp.maximum(jnp.exp(scaled[:, :draft_len] - draft_lse[:, :, None]) - draft_probs, 0.0)
        norm_sum = lax.psum(jnp.sum(excess, axis=-1), 'tp')
        residual = excess / norm_sum[:, :, None]
        return accept, norm_sum, residual, row_lse[:, draft_len]

    return jax.shard_map(
        local_step,
        mesh=mesh,
        in_specs=(P('dp', None, None), P(), P(None, 'tp'), P('dp', None, 'tp'), P('dp', None), P('dp')),
        out_specs=(P('dp', None), P('dp', None), P('dp', None, 'tp'), P('dp')),
        check_vma=False,
    )
```

profile of v0, /device:TPU:0, one launch (start us, length us, event | category | flops | bytes accessed | tf_op | source)
XLA Modules:
  0.0 127.8 jit_solution(9665682217925226297)
XLA Ops:
  0.6 0.7 fusion.16
  1.4 0.1 copy.44
  1.5 0.1 reshape.58
  1.6 0.0 copy-start
  1.6 0.0 copy-start.1
  1.6 0.0 copy-start.4
  1.6 3.8 %gather_fusion.1 = f32[192]{0:T(256)S(1)} fusion(f32[64,3,18992]{2,0,1:T(8,128)} %param.11, s32[192]{0:T(256)S(1)} %reshape.58), kind=kCustom, calls=%fused_computation.1.clone | custom fusion | bytes 3840 | tf_op jit(solution)/shard_map/jit(take_along_axis)/gather | solution.py:22
  5.4 0.1 reshape.67
  5.5 0.1 copy.47
  5.6 0.0 copy-done
  5.6 0.5 fusion.6
  6.1 0.0 copy-done.1
  6.1 0.5 fusion.8
  6.6 0.0 copy-done.4
  6.6 30.6 %fusion.17 = (f32[64,4]{0,1:T(4,128)S(1)}, f32[64,4,18992]{2,0,1:T(8,128)}) fusion(f32[64]{0:T(128)S(1)} %copy-done.4, bf16[1536,18992]{0,1:T(8,128)(2,1)} %param.10, bf16[64,4,1536]{2,1,0:T(4,128)(2,1)S(1)} %fusion.8), kind=kOutput, calls=%fused_computation.35 | convolution fusion | flops 14945640448 | bytes 78578944 | tf_op jit(solution)/shard_map/cle,ew->clw/dot_general | solution.py:14
  37.3 18.3 %pmax.7 = f32[64,4]{0,1:T(4,128)S(1)} all-reduce(f32[64,4]{0,1:T(4,128)S(1)} %get-tuple-element.21), channel_id=1, replica_groups=mesh['dp'=4,'tp'=8] {'tp'}, use_global_device_ids=true, to_apply=%region_3.5 | all-reduce | flops 256 | bytes 2048 | tf_op jit(solution)/shard_map/pmax | solution.py:16
  55.6 9.3 %exponential_reduce_fusion = f32[64,4]{0,1:T(4,128)S(1)} fusion(f32[64,4,18992]{2,0,1:T(8,128)} %get-tuple-element.22, f32[64,4]{0,1:T(4,128)S(1)} %pmax.7), kind=kLoop, calls=%fused_computation.5 | loop fusion | flops 9723648 | bytes 19449856 | tf_op jit(solution)/shard_map/reduce_sum | solution.py:17
  64.9 13.6 %psum.29 = f32[64,4]{0,1:T(4,128)S(1)} all-reduce(f32[64,4]{0,1:T(4,128)S(1)} %exponential_reduce_fusion), channel_id=1, replica_groups=mesh['dp'=4,'tp'=8] {'tp'}, use_global_device_ids=true, to_apply=%region_5.7 | all-reduce | flops 256 | bytes 2048 | tf_op jit(solution)/shard_map/psum | solution.py:23
  78.4 0.5 slice_bitcast_fusion
  79.0 14.9 %fusion.5 = (f32[64,3]{0,1:T(4,128)S(1)}, f32[64,3,18992]{2,0,1:T(8,128)}) fusion(f32[64,3,18992]{2,0,1:T(8,128)} %param.11, f32[64,3]{0,1:T(4,128)S(1)} %bitcast.29, f32[64,4,18992]{2,0,1:T(8,128)} %get-tuple-element.22), kind=kLoop, calls=%fused_computation.8 | loop fusion | flops 14585664 | bytes 43759104 | tf_op jit(solution)/shard_map/reduce_sum | solution.py:29
  93.9 0.0 copy-start.2
  93.9 3.7 %gather_fusion = f32[192]{0:T(256)S(1)} fusion(f32[64,3,18992]{2,0,1:T(8,128)} %get-tuple-element.20, s32[192]{0:T(256)S(1)} %reshape.58), kind=kCustom, calls=%fused_computation.clone | custom fusion | bytes 3840 | tf_op jit(solution)/shard_map/jit(take_along_axis)/gather | solution.py:21
  97.6 0.1 reshape.61
  97.8 0.1 copy.45
  97.8 0.0 copy-done.2
  97.9 13.9 %all-reduce = (f32[64,3]{0,1:T(4,128)S(1)}, f32[64,3]{0,1:T(4,128)S(1)}, f32[64,3]{0,1:T(4,128)S(1)}) all-reduce(f32[64,3]{0,1:T(4,128)S(1)} %bitcast_select_fusion, f32[64,3]{0,1:T(4,128)S(1)} %get-tuple-element.16, f32[64,3]{0,1:T(4,128)S(1)} %get-tuple-element.19), channel_id=1, replica_groups=mesh['dp'=4,'tp'=8] {'tp'}, use_global_device_ids=true, to_apply=%region_6.8 | all-reduce | flops 576 | bytes 4608 | tf_op jit(solution)/shard_map/psum | solution.py:23
  111.8 0.0 copy-start.3
  111.8 15.4 %broadcast_divide_fusion = f32[64,3,18992]{2,0,1:T(8,128)} fusion(f32[64,3]{0,1:T(4,128)S(1)} %get-tuple-element.15, f32[64,3,18992]{2,0,1:T(8,128)} %param.11, f32[64,3]{0,1:T(4,128)S(1)} %bitcast.30, f32[64,4,18992]{2,0,1:T(8,128)} %get-tuple-element.22), kind=kLoop, calls=%fused_computation.7 | loop fusion | flops 14585856 | bytes 43759104 | tf_op jit(solution)/shard_map/div | solution.py:30
  127.3 0.0 copy-done.3
  127.3 0.6 fusion.15
  (8 shorter events, 0.1 us)
Async XLA Ops:
  1.6 4.0 %copy-start = (bf16[64,4,1536]{2,1,0:T(4,128)(2,1)S(1)}, bf16[64,4,1536]{2,1,0:T(4,128)(2,1)}, u32[]{:S(2)}) copy-start(bf16[64,4,1536]{2,1,0:T(4,128)(2,1)} %param.8) | copy-start | bytes 2359300
  1.6 4.5 %copy-start.1 = (f32[1536]{0:T(1024)S(1)}, f32[1536]{0:T(1024)}, u32[]{:S(2)}) copy-start(f32[1536]{0:T(1024)} %param.9) | copy-start | bytes 18436
  1.6 5.0 %copy-start.4 = (f32[64]{0:T(128)S(1)}, f32[64]{0:T(128)}, u32[]{:S(2)}) copy-start(f32[64]{0:T(128)} %param.13) | copy-start | bytes 772
  93.9 3.9 %copy-start.2 = (s32[64,3]{0,1:T(4,128)S(1)}, s32[64,3]{0,1:T(4,128)}, u32[]{:S(2)}) copy-start(s32[64,3]{0,1:T(4,128)} %param.12) | copy-start | bytes 2308
  111.8 15.5 %copy-start.3 = (f32[64,3]{0,1:T(4,128)}, f32[64,3]{0,1:T(4,128)S(1)}, u32[]{:S(2)}) copy-start(f32[64,3]{0,1:T(4,128)S(1)} %get-tuple-element.15) | copy-start | bytes 2308
where the time goes:
time: 128 us
  blocking collectives  45.8 us (36%)
  other arithmetic  42 us (33%)
  matrix products  30.6 us (24%)
  local copies, waits for them, and re-layouts  8.67 us (7%)
    dot_general x1, matrix products, local_step(): jnp.einsum('cle,ew->clw', normed, w_head, preferred_element_type=jnp.floa...  30.6 us
    psum x2, blocking collectives, local_step(): lax.psum((local_sum, tok_scaled, tok_draft), 'tp')  27.5 us
    pmax x1, blocking collectives, local_step(): row_max = lax.pmax(jnp.max(scaled, axis=-1), 'tp')  18.3 us
    div x1, other arithmetic, local_step(): residual = excess / norm_sum[:, :, None]  15.4 us
    reduce_sum x1, other arithmetic, local_step(): norm_sum = lax.psum(jnp.sum(excess, axis=-1), 'tp')  14.9 us
    reduce_sum x1, other arithmetic, local_step(): local_sum = jnp.sum(jnp.exp(scaled - row_max[:, :, None]), axis=-1)  9.28 us
    gather x5, local copies, waits for them, and re-layouts, local_step(): jnp.take_along_axis(scaled[:, :draft_len], safe_idx, axis=-1)[:, :, 0]  4.16 us
    gather x3, local copies, waits for them, and re-layouts, local_step(): jnp.take_along_axis(draft_probs, safe_idx, axis=-1)[:, :, 0]  3.95 us

commit v1 on v0

v1 whole, which is shorter than its diff:
```python
import functools

import jax
import jax.numpy as jnp
from jax import lax
from jax.experimental import pallas as pl
from jax.experimental.pallas import tpu as pltpu
from jax.sharding import PartitionSpec as P

LOG2E = 1.4426950408889634
LN2 = 0.6931471805599453
MESH = pl.DeviceIdType.MESH
TILE = 512
DEPTH = 9
GROUP = 3
Q_STEPS = 3
LOW = -3.0e38


def _verify_kernel(n, x_ref, k_ref, kp_ref, hit_ref, w_ref, q_ref, z_ref, stat_ref, norm_ref,
                   wbuf, wtail, qbuf, zt, m_ref, l_ref, lse_ref, send1, recv1, send2, recv2,
                   wsem, tsem, qsem, ssem1, rsem1, ssem2, rsem2):
    me = lax.axis_index('tp')
    dp = lax.axis_index('dp')
    vocab = w_ref.shape[0]
    width = w_ref.shape[1]
    rows = x_ref.shape[0]
    seqs = rows // 4
    draft_rows = rows - seqs
    groups = draft_rows // 8
    all_groups = rows // 8
    tiles = vocab // TILE
    tail = vocab - tiles * TILE
    tail_at = tiles * TILE
    lane = lax.broadcasted_iota(jnp.int32, (8, 128), 1)
    sub = lax.broadcasted_iota(jnp.int32, (8, 128), 0)

    def q_copy(g):
        at = pl.ds(pl.multiple_of(g * 8, 8), 8)
        return pltpu.make_async_copy(q_ref.at[at, :], qbuf.at[at, :], qsem.at[g])

    order = lambda r: lax.rem(r + tiles - 1, tiles)

    def w_copy(r):
        slot = lax.rem(r, DEPTH)
        at = pl.ds(pl.multiple_of(order(r) * TILE, TILE), TILE)
        return pltpu.make_async_copy(w_ref.at[at, :], wbuf.at[slot], wsem.at[slot])

    tail_copy = pltpu.make_async_copy(w_ref.at[pl.ds(tail_at, tail), :], wtail, tsem)
    tail_copy.start()
    for i in range(DEPTH):
        w_copy(i).start()

    barrier = pltpu.get_barrier_semaphore()
    for d in range(1, n):
        pl.semaphore_signal(barrier, inc=1, device_id=(dp, lax.rem(me + d, n)), device_id_type=MESH)

    m_ref[...] = jnp.full_like(m_ref, LOW)
    l_ref[...] = jnp.zeros_like(l_ref)

    def dot(w):
        return lax.dot_general(x_ref[...], w, (((1,), (1,)), ((), ())), preferred_element_type=jnp.float32)

    def process(src, tile):
        base = tile * TILE
        for g in range(all_groups):
            at = slice(g * 8, g * 8 + 8)
            k = k_ref[at, :]
            old = m_ref[at, :]
            parts = [src[at, c * 128:c * 128 + 128] for c in range(TILE // 128)]
            new = old
            for c, v in enumerate(parts):
                new = jnp.maximum(new, v)
                if g < groups:
                    z_ref[at, pl.ds(pl.multiple_of(base + c * 128, 128), 128)] = v
            total = l_ref[at, :] * jnp.exp2((old - new) * k)
            for v in parts:
                total = total + jnp.exp2((v - new) * k)
            m_ref[at, :] = new
            l_ref[at, :] = total

    def step(r, p, carry, refill=True):
        for t in range(GROUP):
            w_copy(r + t).wait()

        for t in range(GROUP if refill else 0):
            @pl.when(r - GROUP + t + DEPTH < tiles)
            def _():
                w_copy(r - GROUP + t + DEPTH).start()

        first = (r - 1) // GROUP - (steps - Q_STEPS)
        per = groups // Q_STEPS

        @pl.when(first >= 0)
        def _():
            for j in range(per):
                q_copy(first * per + j).start()

        for t in range(GROUP):
            zt[p, t] = dot(wbuf[lax.rem(r + t, DEPTH)])
            if t == 0:
                process(zt.at[1 - p, carry], order(r - 1))
            else:
                process(zt.at[p, t - 1], order(r + t - 1))

    steps = (tiles - 1) // GROUP
    tail_copy.wait()
    z_tail = dot(wtail[...])
    z_ref[:, tail_at:tail_at + tail] = z_tail[:draft_rows]
    m_ref[:, :tail] = z_tail
    l_ref[:, :tail] = jnp.ones_like(z_tail)
    w_copy(0).wait()
    zt[1, 0] = dot(wbuf[0])
    w_copy(DEPTH).start()

    step(1, 0, 0, refill=False)

    @pl.loop(0, (steps - 1) // 2)
    def _(t):
        r = 1 + GROUP * (1 + 2 * t)
        step(r, 1, GROUP - 1)
        step(r + GROUP, 0, GROUP - 1)

    last = 0
    if steps % 2 == 0:
        step(1 + GROUP * (steps - 1), 1, GROUP - 1)
        last = 1
    process(zt.at[last, GROUP - 1], order(tiles - 1))

    def pack(acc, g, col):
        return jnp.where((lane == g) | (lane == g + 32), col, acc)

    packed_m = jnp.zeros((8, 128), jnp.float32)
    packed_l = jnp.zeros((8, 128), jnp.float32)
    for g in range(all_groups):
        at = slice(g * 8, g * 8 + 8)
        m = m_ref[at, :]
        top = jnp.max(m, axis=1, keepdims=True)
        total = jnp.sum(l_ref[at, :] * jnp.exp2((m - top) * k_ref[at, :]), axis=1, keepdims=True)
        packed_m = pack(packed_m, g, top)
        packed_l = pack(packed_l, g, total)
    send1[0] = packed_m
    send1[1] = packed_l
    recv1[me, 0] = packed_m
    recv1[me, 1] = packed_l

    pl.semaphore_wait(barrier, n - 1)

    def share(src, dst, ssem, rsem):
        copies = []
        for d in range(1, n):
            copy = pltpu.make_async_remote_copy(
                src_ref=src, dst_ref=dst.at[me], send_sem=ssem.at[d], recv_sem=rsem.at[me],
                device_id=(dp, lax.rem(me + d, n)), device_id_type=MESH)
            copy.start()
            copies.append(copy)
        return copies

    def collect(src, dst, ssem, rsem):
        for d in range(1, n):
            peer = lax.rem(me + d, n)
            pltpu.make_async_remote_copy(
                src_ref=src, dst_ref=dst.at[peer], send_sem=ssem.at[d], recv_sem=rsem.at[peer],
                device_id=(dp, peer), device_id_type=MESH).wait_recv()

    copies1 = share(send1, recv1, ssem1, rsem1)

    def gather(ref, wait=None):
        def one(g, packed):
            if wait is not None:
                wait(g)
            at = pl.ds(pl.multiple_of(g * 8, 8), 8)
            hit = hit_ref[at, :]
            got = [jnp.zeros((8, 128), jnp.float32) for _ in range(4)]
            for c in range(vocab // 128):
                got[c % 4] = jnp.where(hit - c * 128 == lane, ref[at, c * 128:c * 128 + 128], got[c % 4])
            edge = (vocab // 128) * 128
            rest = vocab - edge
            last = jnp.where(hit[:, :rest] - edge == lane[:, :rest], ref[at, edge:], 0.0)
            col = jnp.sum((got[0] + got[1]) + (got[2] + got[3]), axis=1, keepdims=True)
            return pack(packed, g, col + jnp.sum(last, axis=1, keepdims=True))

        return lax.fori_loop(0, groups, one, jnp.zeros((8, 128), jnp.float32))

    tok_z = gather(z_ref)
    tok_q = gather(qbuf, lambda g: q_copy(g).wait())

    collect(send1, recv1, ssem1, rsem1)
    kp = kp_ref[...]
    top = recv1[0, 0]
    for i in range(1, n):
        top = jnp.maximum(top, recv1[i, 0])
    total = jnp.zeros((8, 128), jnp.float32)
    for i in range(n):
        total = total + recv1[i, 1] * jnp.exp2((recv1[i, 0] - top) * kp)
    lse = top * kp + jnp.log(total) * LOG2E
    stat_ref[1] = lse * LN2
    for g in range(groups):
        col = jnp.sum(jnp.where(lane == g, lse, 0.0), axis=1, keepdims=True)
        lse_ref[g * 8:g * 8 + 8, :] = jnp.broadcast_to(col, (8, 128))

    full = vocab // 128

    def excess(g, packed):
        at = pl.ds(pl.multiple_of(g * 8, 8), 8)
        k = k_ref[at, :]
        base = lse_ref[at, :]
        sums = [jnp.zeros((8, 128), jnp.float32) for _ in range(4)]
        for c in range(full):
            cols = slice(c * 128, c * 128 + 128)
            e = jnp.maximum(jnp.exp2(z_ref[at, cols] * k - base) - qbuf[at, cols], 0.0)
            z_ref[at, cols] = e
            sums[c % 4] = sums[c % 4] + e
        rest = vocab - full * 128
        cols = slice(full * 128, vocab)
        e = jnp.maximum(jnp.exp2(z_ref[at, cols] * k[:, :rest] - base[:, :rest]) - qbuf[at, cols], 0.0)
        z_ref[at, cols] = e
        col = jnp.sum((sums[0] + sums[1]) + (sums[2] + sums[3]), axis=1, keepdims=True)
        col = col + jnp.sum(e, axis=1, keepdims=True)
        return jnp.where(lane == g, col, packed)

    packed = lax.fori_loop(0, groups, excess, jnp.zeros((8, 128), jnp.float32))
    ones = jnp.where(tok_q > 0, tok_q, 1.0)
    accept = jnp.where(tok_q > 0, jnp.minimum(1.0, jnp.exp2(tok_z * kp - lse) / ones), 0.0)
    packed = jnp.where((lane >= 32) & (lane < 64), accept, packed)
    send2[...] = packed
    recv2[me] = packed
    copies2 = share(send2, recv2, ssem2, rsem2)
    collect(send2, recv2, ssem2, rsem2)
    total = recv2[0]
    for i in range(1, n):
        total = total + recv2[i]
    stat_ref[0] = total
    inv = 1.0 / total
    for g in range(groups):
        col = jnp.sum(jnp.where(lane == g, inv, 0.0), axis=1, keepdims=True)
        norm_ref[g * 8:g * 8 + 8, :] = jnp.broadcast_to(col, (8, 128))
    for copy in copies1 + copies2:
        copy.wait_send()


def _scale_kernel(e_ref, norm_ref, o_ref):
    rows, vocab = o_ref.shape
    step = pl.program_id(0)
    full = vocab // 128
    for g in range(rows // 8):
        at = pl.ds(pl.multiple_of(step * rows + g * 8, 8), 8)
        out = slice(g * 8, g * 8 + 8)
        inv = norm_ref[at, :]
        for c in range(full):
            cols = slice(c * 128, c * 128 + 128)
            o_ref[out, cols] = e_ref[at, cols] * inv
        cols = slice(full * 128, vocab)
        o_ref[out, cols] = e_ref[at, cols] * inv[:, :vocab - full * 128]


def solution(mesh):
    n = mesh.shape['tp']

    def local_step(hidden, norm_gain, w_head, draft_probs, draft_tokens, temperature):
        seqs, positions, width = hidden.shape
        vocab = w_head.shape[1]
        rows = seqs * positions
        draft = positions - 1
        draft_rows = seqs * draft
        h = hidden.astype(jnp.float32)
        inv_rms = lax.rsqrt(jnp.mean(h * h, axis=-1, keepdims=True) + 1e-5)
        x = (h * inv_rms * norm_gain).astype(jnp.bfloat16)
        x = x.transpose(1, 0, 2).reshape(rows, width)
        k = jnp.tile(LOG2E / temperature, positions)
        k_cols = jnp.broadcast_to(k[:, None], (rows, 128))
        kp = jnp.tile(k.reshape(rows // 8, 8).T, (1, 4))
        tok = draft_tokens.T.reshape(draft_rows) - lax.axis_index('tp') * vocab
        hit = jnp.where((tok >= 0) & (tok < vocab), tok, -1)
        hit = jnp.broadcast_to(hit[:, None], (draft_rows, 128))
        q = draft_probs.transpose(1, 0, 2).reshape(draft_rows, vocab)
        vmem = pl.BlockSpec(memory_space=pltpu.VMEM)
        hbm = pl.BlockSpec(memory_space=pl.ANY)
        f32 = jnp.float32
        z, stat, norm = pl.pallas_call(
            functools.partial(_verify_kernel, n),
            out_shape=(pltpu.VMEM((draft_rows, vocab), f32),
                       jax.ShapeDtypeStruct((2, 8, 128), f32),
                       pltpu.VMEM((draft_rows, 128), f32)),
            in_specs=[vmem, vmem, vmem, vmem, hbm, hbm],
            out_specs=(vmem, vmem, vmem),
            scratch_shapes=[
                pltpu.VMEM((DEPTH, TILE, width), jnp.bfloat16),
                pltpu.VMEM((vocab % TILE, width), jnp.bfloat16),
                pltpu.VMEM((draft_rows, vocab), f32),
                pltpu.VMEM((2, GROUP, rows, TILE), f32),
                pltpu.VMEM((rows, 128), f32),
                pltpu.VMEM((rows, 128), f32),
                pltpu.VMEM((draft_rows, 128), f32),
                pltpu.VMEM((2, 8, 128), f32),
                pltpu.VMEM((n, 2, 8, 128), f32),
                pltpu.VMEM((8, 128), f32),
                pltpu.VMEM((n, 8, 128), f32),
                pltpu.SemaphoreType.DMA((DEPTH,)),
                pltpu.SemaphoreType.DMA,
                pltpu.SemaphoreType.DMA((draft_rows // 8,)),
                pltpu.SemaphoreType.DMA((n,)),
                pltpu.SemaphoreType.DMA((n,)),
                pltpu.SemaphoreType.DMA((n,)),
                pltpu.SemaphoreType.DMA((n,)),
            ],
            compiler_params=pltpu.CompilerParams(
                collective_id=0, has_side_effects=True, vmem_limit_bytes=48 * 2**20),
            name='verify',
        )(x, k_cols, kp, hit, w_head.T, q)
        block = 16
        residual = pl.pallas_call(
            _scale_kernel,
            out_shape=jax.ShapeDtypeStruct((draft_rows, vocab), f32),
            grid=(draft_rows // block,),
            in_specs=[vmem, vmem],
            out_specs=pl.BlockSpec((block, vocab), lambda i: (i, 0)),
            compiler_params=pltpu.CompilerParams(vmem_limit_bytes=8 * 2**20),
            name='scale',
        )(z, norm)
        groups = draft_rows // 8
        norm_sum = stat[0, :, :groups].T.reshape(draft, seqs).T
        accept = stat[0, :, 32:32 + groups].T.reshape(draft, seqs).T
        bonus = stat[1, :, groups:rows // 8].T.reshape(seqs)
        return accept, norm_sum, residual.reshape(draft, seqs, vocab).transpose(1, 0, 2), bonus

    return jax.shard_map(
        local_step,
        mesh=mesh,
        in_specs=(P('dp', None, None), P(), P(None, 'tp'), P('dp', None, 'tp'), P('dp', None), P('dp')),
        out_specs=(P('dp', None), P('dp', None), P('dp', None, 'tp'), P('dp')),
        check_vma=False,
    )
```

time: 128 us -> 62.8 us (0.49)
  Pallas kernels: 0 us -> 51.7 us
  blocking collectives: 45.8 us -> 0 us
  other arithmetic: 42 us -> 4.23 us
  matrix products: 30.6 us -> 0 us
  local copies, waits for them, and re-layouts: 8.67 us -> 5.86 us
    pallas_call x0 -> x2, Pallas kernels: none -> 51.7 us  [the longest x1 44.7 us: local_step(): pl.pallas_call(functools.partial(_verify_kernel, n), out_shape=(pltpu.VME...]
    dot_general x1 -> x0, matrix products: 30.6 us -> none  [local_step(): jnp.einsum('cle,ew->clw', normed, w_head, preferred_element_type=jnp.floa...]
    psum x2 -> x0, blocking collectives: 27.5 us -> none  [local_step(): lax.psum((local_sum, tok_scaled, tok_draft), 'tp')]
    reduce_sum x3 -> x1, other arithmetic: 24.7 us -> 1.62 us  [local_step(): inv_rms = lax.rsqrt(jnp.mean(h * h, axis=-1, keepdims=True) + 1e-05)]
    pmax x1 -> x0, blocking collectives: 18.3 us -> none  [local_step(): row_max = lax.pmax(jnp.max(scaled, axis=-1), 'tp')]
    div x1, other arithmetic: 15.4 us -> 0.73 us  [local_step(): k = jnp.tile(LOG2E / temperature, positions)]
    gather x8 -> x0, local copies, waits for them, and re-layouts: 8.11 us -> none  [the longest x5 4.16 us: local_step(): jnp.take_along_axis(scaled[:, :draft_len], safe_idx, axis=-1)[:, :, 0]]
    reshape x0 -> x3, local copies, waits for them, and re-layouts: none -> 1.92 us  [the longest x1 0.66 us: local_step(): norm_sum = stat[0, :, :groups].T.reshape(draft, seqs).T]
where the time goes in v1:
time: 62.8 us; the launch traced here: 62.5 us
  Pallas kernels  51.7 us (82%)
  local copies, waits for them, and re-layouts  5.86 us (9%)
  other arithmetic  4.23 us (7%)
  between operations  0.68 us (1%)
    pallas_call x1, Pallas kernels, local_step(): pl.pallas_call(functools.partial(_verify_kernel, n), out_shape=(pltpu.VME...  44.7 us
    pallas_call x1, Pallas kernels, local_step(): pl.pallas_call(_scale_kernel, out_shape=jax.ShapeDtypeStruct((draft_rows,...  7.06 us
    reduce_sum x1, other arithmetic, local_step(): inv_rms = lax.rsqrt(jnp.mean(h * h, axis=-1, keepdims=True) + 1e-05)  1.62 us

profile of v1, /device:TPU:0, one launch (start us, length us, event | category | flops | bytes accessed | tf_op | source)
XLA Modules:
  0.0 62.5 jit_solution(13899043378214739163)
XLA Ops:
  0.6 0.0 copy-start
  0.6 0.7 %broadcast_divide_fusion = f32[64]{0:T(128)S(1)} fusion(f32[64]{0:T(128)} %param.11), kind=kLoop, calls=%fused_computation.12 | loop fusion | flops 64 | bytes 512 | tf_op jit(solution)/shard_map/div | solution.py:270
  1.4 0.7 %subtract_bitcast_fusion = s32[3,64]{1,0:T(4,128)S(1)} fusion(s32[64,3]{0,1:T(4,128)} %param.10, s32[]{:T(128)S(6)} %mul.27), kind=kLoop, calls=%fused_computation.10 | loop fusion | flops 192 | bytes 1540 | tf_op jit(solution)/shard_map/sub | solution.py:273
  2.1 0.1 sub.19
  2.2 0.1 broadcast_in_dim.10
  2.2 0.1 tile.22
  2.3 0.1 copy.27
  2.4 0.1 tile.24
  2.5 0.7 %tile.26.kp_ref = f32[8,128]{1,0:T(8,128)} reshape(f32[8,4,32]{2,1,0:T(4,128)S(1)} %tile.25) | data formatting | bytes 8192 | tf_op jit(solution)/shard_map/tile | solution.py:272
  3.2 1.6 %fusion = f32[64,4]{1,0:T(8,128)S(1)} fusion(bf16[64,4,1536]{2,1,0:T(4,128)(2,1)} %param.6), kind=kLoop, calls=%fused_computation.2 | loop fusion | flops 1179392 | bytes 787456 | tf_op jit(solution)/shard_map/reduce_sum | solution.py:267
  4.8 0.7 %broadcast_in_dim.22.hit_ref = s32[192,128]{1,0:T(8,128)} broadcast(s32[192]{0:T(256)S(1)} %and_select_fusion), dimensions={0} | broadcast | bytes 99072 | tf_op jit(solution)/shard_map/broadcast_in_dim | solution.py:275
  5.5 0.7 %broadcast_in_dim.20.k_ref = f32[256,128]{1,0:T(8,128)} broadcast(f32[256]{0:T(256)S(1)} %broadcast_in_dim.10), dimensions={0} | broadcast | bytes 132096 | tf_op jit(solution)/shard_map/broadcast_in_dim | solution.py:271
  6.3 0.0 copy-done
  6.3 1.2 %fusion.3 = bf16[4,64,1536]{2,0,1:T(4,128)(2,1)S(1)} fusion(bf16[64,4,1536]{2,1,0:T(4,128)(2,1)S(1)} %copy-done, f32[1536]{0:T(1024)} %param.7, f32[64,4]{1,0:T(8,128)S(1)} %add_rsqrt_fusion), kind=kLoop, calls=%fused_computation.5 | loop fusion | flops 1572864 | bytes 1580032 | tf_op jit(solution)/shard_map/transpose | solution.py:269
  7.5 1.0 %copy.26 = bf16[4,64,1536]{2,1,0:T(8,128)(2,1)} copy(bf16[4,64,1536]{2,0,1:T(4,128)(2,1)S(1)} %fusion.3) | data formatting | bytes 1572864 | tf_op jit(solution)/shard_map/transpose | solution.py:269
  8.5 44.7 %verify.1 = (f32[192,18992]{1,0:T(8,128)S(1)}, f32[2,8,128]{2,1,0:T(8,128)}, f32[192,128]{1,0:T(8,128)S(1)}) custom-call(bf16[256,1536]{1,0:T(8,128)(2,1)} %bitcast.32, f32[256,128]{1,0:T(8,128)} %broadcast_in_dim.20.k_ref, f32[8,128]{1,0:T(8,128)} %tile.26.kp_ref, s32[192,128]{1,0:T(8,128)} %broadcast_in_dim.22.hit_ref, bf16[18992,1536]{1,0:T(8,128)(2,1)} %bitcast.29, ...), custom_call_target="tpu_custom_call" | custom-call | tf_op jit(solution)/shard_map/verify/pallas_call | solution.py:280
  53.2 0.0 copy-start.1
  53.2 7.1 %scale.1 = f32[192,18992]{1,0:T(8,128)} custom-call(f32[192,18992]{1,0:T(8,128)S(1)} %get-tuple-element.8.e_ref, f32[192,128]{1,0:T(8,128)S(1)} %get-tuple-element.9.norm_ref), custom_call_target="tpu_custom_call" | custom-call | tf_op jit(solution)/shard_map/scale/pallas_call | solution.py:312
  60.2 0.0 copy-done.1
  60.2 0.1 slice_bitcast_fusion
  60.3 0.1 copy.30
  60.4 0.6 reshape.60
  61.0 0.1 slice_bitcast_fusion.1
  61.0 0.1 copy.29
  61.1 0.7 %reshape.58 = f32[3,64]{1,0:T(4,128)} reshape(f32[24,8]{1,0:T(8,128)S(1)} %copy.29) | data formatting | bytes 1536 | tf_op jit(solution)/shard_map/reshape | solution.py:322
  61.8 0.1 copy.28
  61.8 0.7 %reshape.57 = f32[3,64]{1,0:T(4,128)} reshape(f32[24,8]{1,0:T(8,128)S(1)} %copy.28) | data formatting | bytes 1536 | tf_op jit(solution)/shard_map/reshape | solution.py:323
  (5 shorter events, 0.0 us)
Async XLA Ops:
  0.6 5.6 %copy-start = (bf16[64,4,1536]{2,1,0:T(4,128)(2,1)S(1)}, bf16[64,4,1536]{2,1,0:T(4,128)(2,1)}, u32[]{:S(2)}) copy-start(bf16[64,4,1536]{2,1,0:T(4,128)(2,1)} %param.6) | copy-start | bytes 2359300
  53.2 7.1 %copy-start.1 = (f32[2,8,128]{2,1,0:T(8,128)S(1)}, f32[2,8,128]{2,1,0:T(8,128)}, u32[]{:S(2)}) copy-start(f32[2,8,128]{2,1,0:T(8,128)} %get-tuple-element.7) | copy-start | bytes 24580

commit v2 on v0

v2 whole, which is shorter than its diff:
```python
import functools

import jax
import jax.numpy as jnp
from jax import lax
from jax.experimental import pallas as pl
from jax.experimental.pallas import tpu as pltpu
from jax.sharding import PartitionSpec as P

LOG2E = 1.4426950408889634
LN2 = 0.6931471805599453
MESH = pl.DeviceIdType.MESH
TILE = 512
DEPTH = 10
LOW = -3.0e38


def _pack(packed, g, col):
    lane = lax.broadcasted_iota(jnp.int32, (8, 128), 1)
    return jnp.where((lane == g) | (lane == g + 32), col, packed)


def _stream_kernel(h_ref, gain_ref, temp_ref, tok_ref, w_ref,
                   z_ref, ml_ref, tok_z_ref, k_ref, kp_ref, hit_ref,
                   hbuf, gbuf, tbuf, dbuf, hp_ref, x_ref, tz_ref, wbuf, wtail, m_ref, l_ref,
                   wsem, tsem, isem):
    me = lax.axis_index('tp')
    vocab = w_ref.shape[0]
    width = w_ref.shape[1]
    seqs = h_ref.shape[0]
    rows = seqs * 4
    per = seqs // 8
    draft_rows = rows - seqs
    groups = draft_rows // 8
    all_groups = rows // 8
    tiles = vocab // TILE
    tail = vocab - tiles * TILE
    tail_at = tiles * TILE
    chunks = width // 256
    lane = lax.broadcasted_iota(jnp.int32, (8, 128), 1)
    sub = lax.broadcasted_iota(jnp.int32, (8, 128), 0)

    def w_copy(tile):
        slot = lax.rem(tile, DEPTH)
        return pltpu.make_async_copy(
            w_ref.at[pl.ds(pl.multiple_of(tile * TILE, TILE), TILE), :], wbuf.at[slot], wsem.at[slot])

    first_copies = [pltpu.make_async_copy(a, b, isem.at[i]) for i, (a, b) in enumerate(
        ((h_ref, hbuf), (temp_ref, tbuf), (gain_ref, gbuf), (tok_ref, dbuf)))]
    for copy in first_copies:
        copy.start()
    tail_copy = pltpu.make_async_copy(w_ref.at[pl.ds(tail_at, tail), :], wtail.at[pl.ds(0, tail), :], tsem)
    tail_copy.start()
    for i in range(DEPTH - 1):
        w_copy(i).start()

    m_ref[...] = jnp.full_like(m_ref, LOW)
    l_ref[...] = jnp.zeros_like(l_ref)
    tz_ref[...] = jnp.zeros_like(tz_ref)
    wtail[tail:, :] = jnp.zeros((wtail.shape[0] - tail, width), wtail.dtype)

    for copy in first_copies[1:]:
        copy.wait()

    def column(row, g):
        picked = jnp.where(lane[:, :seqs] == g * 8 + sub[:, :seqs], jnp.broadcast_to(row, (8, seqs)), 0.0)
        return jnp.sum(picked, axis=1, keepdims=True)

    kp = jnp.zeros((8, 128), jnp.float32)
    for g in range(per):
        k = jnp.broadcast_to(LOG2E / column(tbuf[...], g), (8, 128))
        k_ref[g * 8:g * 8 + 8, :] = k
        kp = jnp.where(lax.rem(lane, per) == g, k, kp)
    for j in range(3):
        row = (dbuf[j:j + 1, :] - me * vocab).astype(jnp.float32)
        for g in range(per):
            at = slice(j * seqs + g * 8, j * seqs + g * 8 + 8)
            hit_ref[at, :] = jnp.broadcast_to(column(row, g), (8, 128)).astype(jnp.int32)
    kp_ref[...] = kp
    first_copies[0].wait()

    def run(*accs):
        def acc(q, p, b):
            return accs[(q * 2 + p) * 4 + b]

        def accumulate(q, p, c):
            for b in range(4):
                pltpu.matmul_acc_lhs(
                    acc(q, p, b), x_ref[b * seqs:(b + 1) * seqs, c * 256:(c + 1) * 256],
                    load_staged_rhs=c % 2 if b == 0 else None)

        def push(tile, q, c):
            slot = lax.rem(tile, DEPTH)
            pltpu.matmul_push_rhs(
                wbuf[slot, q * 256:(q + 1) * 256, c * 256:(c + 1) * 256],
                staging_register=c % 2, mxu_index=q, transpose=True)

        cols = lax.broadcasted_iota(jnp.int32, (seqs, 128), 1)

        def update(b, parts, base):
            at = slice(b * seqs, (b + 1) * seqs)
            k = k_ref[...]
            old = m_ref[at, :]
            new = old
            if b < 3:
                hit = hit_ref[at, :] - base
                got = tz_ref[at, :]
                for i, v in enumerate(parts):
                    got = jnp.where(hit == cols + i * 128, v, got)
                tz_ref[at, :] = got
            for v in parts:
                new = jnp.maximum(new, v)
            total = l_ref[at, :] * jnp.exp2((old - new) * k)
            for v in parts:
                total = total + jnp.exp2((v - new) * k)
            m_ref[at, :] = new
            l_ref[at, :] = total

        def drain(tile, p, b):
            parts = []
            for q in range(2):
                v = pltpu.matmul_pop(acc(q, p, b))
                if b < 3:
                    at = pl.ds(pl.multiple_of(tile * TILE + q * 256, 256), 256)
                    z_ref[b * seqs:(b + 1) * seqs, at] = v
                parts += [v[:, :128], v[:, 128:]]
            update(b, parts, tile * TILE)

        def drain_tail(p, b):
            v = pltpu.matmul_pop(acc(0, p, b))
            if b < 3:
                z_ref[b * seqs:(b + 1) * seqs, tail_at:tail_at + tail] = v[:, :tail]
            update(b, [jnp.where(cols < tail, v[:, :128], LOW)], tail_at)

        def step(tile, p, last=False, first=False, refill=None):
            if not last:
                w_copy(tile + 1).wait()
            if refill is not None:
                refill()
            for c in range(chunks):
                for q in range(2):
                    accumulate(q, p, c)
                for q in range(2):
                    if c + 1 < chunks:
                        push(tile, q, c + 1)
                    elif not last:
                        push(tile + 1, q, 0)
                if 1 <= c <= 4:
                    if first:
                        drain_tail(1 - p, c - 1)
                    else:
                        drain(tile - 1, 1 - p, c - 1)

        c_of = lax.broadcasted_iota(jnp.int32, (seqs, 256), 1)
        r_of = lax.broadcasted_iota(jnp.int32, (seqs, 256), 0)
        for c in range(chunks):
            flat = hbuf[:, :, c * 256:(c + 1) * 256].reshape(rows, 256)
            pltpu.matmul_push_rhs(flat, staging_register=(c // 2) % 2, mxu_index=c % 2)
            for b in range(4):
                pick = jnp.where(c_of == r_of * 4 + b, 1.0, 0.0).astype(jnp.bfloat16)
                pltpu.matmul_acc_lhs(acc(c % 2, (c // 2) % 2, b), pick,
                                     load_staged_rhs=(c // 2) % 2 if b == 0 else None)
            for b in range(4):
                hp_ref[b * seqs:(b + 1) * seqs, c * 256:(c + 1) * 256] = pltpu.matmul_pop(acc(c % 2, (c // 2) % 2, b))
        gain = gbuf[...]
        for g in range(all_groups // 2):
            at = slice(g * 16, g * 16 + 16)
            h = hp_ref[at, :]
            inv_rms = lax.rsqrt(jnp.sum(h * h, axis=1, keepdims=True) * (1.0 / width) + 1e-5)
            x_ref[at, :] = (h * inv_rms * gain).astype(jnp.bfloat16)

        tail_copy.wait()
        for c in range(chunks):
            pltpu.matmul_push_rhs(wtail[:, c * 256:(c + 1) * 256], staging_register=c % 2, mxu_index=0, transpose=True)
            accumulate(0, 1, c)
        w_copy(0).wait()
        for q in range(2):
            push(0, q, 0)
        step(0, 0, first=True, refill=lambda: w_copy(DEPTH - 1).start())

        def refill_at(tile):
            @pl.when(tile + DEPTH - 1 < tiles)
            def _():
                w_copy(tile + DEPTH - 1).start()

        @pl.loop(0, (tiles - 3) // 2)
        def _(t):
            tile = 1 + 2 * t
            step(tile, 1, refill=lambda: refill_at(tile))
            step(tile + 1, 0, refill=lambda: refill_at(tile + 1))

        step(tiles - 2, 1)
        step(tiles - 1, 0, last=True)
        for b in range(4):
            drain(tiles - 1, 0, b)

    pl.run_scoped(run, *[pltpu.ACC(q)((seqs, 256), jnp.float32) for q in range(2) for _ in range(8)])

    packed_m = jnp.zeros((8, 128), jnp.float32)
    packed_l = jnp.zeros((8, 128), jnp.float32)
    tok_z = jnp.zeros((8, 128), jnp.float32)
    for g in range(all_groups):
        at = slice(g * 8, g * 8 + 8)
        m = m_ref[at, :]
        top = jnp.max(m, axis=1, keepdims=True)
        k = k_ref[g % per * 8:g % per * 8 + 8, :]
        total = jnp.sum(l_ref[at, :] * jnp.exp2((m - top) * k), axis=1, keepdims=True)
        packed_m = _pack(packed_m, g, top)
        packed_l = _pack(packed_l, g, total)
        if g < groups:
            tok_z = _pack(tok_z, g, jnp.sum(tz_ref[at, :], axis=1, keepdims=True))
    ml_ref[0] = packed_m
    ml_ref[1] = packed_l
    tok_z_ref[...] = tok_z


def _exchange_kernel(n, z_ref, ml_ref, tok_z_ref, k_ref, kp_ref, hit_ref, q_ref, e_ref, stat_ref, norm_ref,
                     lse_ref, recv1, send2, recv2, qsem, ssem1, rsem1, ssem2, rsem2):
    me = lax.axis_index('tp')
    dp = lax.axis_index('dp')
    draft_rows, vocab = q_ref.shape
    groups = draft_rows // 8
    per = k_ref.shape[0] // 8
    full = vocab // 128
    rest = vocab - full * 128
    edge = slice(full * 128, vocab)
    lane = lax.broadcasted_iota(jnp.int32, (8, 128), 1)

    def q_copy(g):
        at = pl.ds(pl.multiple_of(g * 8, 8), 8)
        return pltpu.make_async_copy(q_ref.at[at, :], e_ref.at[at, :], qsem.at[g])

    barrier = pltpu.get_barrier_semaphore()
    for d in range(1, n):
        pl.semaphore_signal(barrier, inc=1, device_id=(dp, lax.rem(me + d, n)), device_id_type=MESH)
    for g in range(groups):
        q_copy(g).start()
    recv1[me] = ml_ref[...]
    pl.semaphore_wait(barrier, n - 1)

    def share(src, dst, ssem, rsem):
        copies = []
        for d in range(1, n):
            copy = pltpu.make_async_remote_copy(
                src_ref=src, dst_ref=dst.at[me], send_sem=ssem.at[d], recv_sem=rsem.at[me],
                device_id=(dp, lax.rem(me + d, n)), device_id_type=MESH)
            copy.start()
            copies.append(copy)
        return copies

    def collect(src, dst, ssem, rsem):
        for d in range(1, n):
            peer = lax.rem(me + d, n)
            pltpu.make_async_remote_copy(
                src_ref=src, dst_ref=dst.at[peer], send_sem=ssem.at[d], recv_sem=rsem.at[peer],
                device_id=(dp, peer), device_id_type=MESH).wait_recv()

    copies1 = share(ml_ref, recv1, ssem1, rsem1)

    def gather(g, packed):
        q_copy(g).wait()
        at = pl.ds(pl.multiple_of(g * 8, 8), 8)
        hit = hit_ref[at, :]
        got = [jnp.zeros((8, 128), jnp.float32) for _ in range(4)]
        for c in range(full):
            got[c % 4] = jnp.where(hit - c * 128 == lane, e_ref[at, c * 128:c * 128 + 128], got[c % 4])
        last = jnp.where(hit[:, :rest] - full * 128 == lane[:, :rest], e_ref[at, edge], 0.0)
        col = jnp.sum((got[0] + got[1]) + (got[2] + got[3]), axis=1, keepdims=True)
        return _pack(packed, g, col + jnp.sum(last, axis=1, keepdims=True))

    tok_q = lax.fori_loop(0, groups, gather, jnp.zeros((8, 128), jnp.float32))

    collect(ml_ref, recv1, ssem1, rsem1)
    kp = kp_ref[...]
    top = recv1[0, 0]
    for i in range(1, n):
        top = jnp.maximum(top, recv1[i, 0])
    total = jnp.zeros((8, 128), jnp.float32)
    for i in range(n):
        total = total + recv1[i, 1] * jnp.exp2((recv1[i, 0] - top) * kp)
    lse = top * kp + jnp.log(total) * LOG2E
    stat_ref[1] = lse * LN2
    for g in range(groups):
        col = jnp.sum(jnp.where(lane == g, lse, 0.0), axis=1, keepdims=True)
        lse_ref[g * 8:g * 8 + 8, :] = jnp.broadcast_to(col, (8, 128))

    def excess(g, packed):
        at = pl.ds(pl.multiple_of(g * 8, 8), 8)
        k = k_ref[pl.ds(pl.multiple_of(lax.rem(g, per) * 8, 8), 8), :]
        base = lse_ref[at, :]
        sums = [jnp.zeros((8, 128), jnp.float32) for _ in range(4)]
        for c in range(full):
            cols = slice(c * 128, c * 128 + 128)
            e = jnp.maximum(jnp.exp2(z_ref[at, cols] * k - base) - e_ref[at, cols], 0.0)
            e_ref[at, cols] = e
            sums[c % 4] = sums[c % 4] + e
        e = jnp.maximum(jnp.exp2(z_ref[at, edge] * k[:, :rest] - base[:, :rest]) - e_ref[at, edge], 0.0)
        e_ref[at, edge] = e
        col = jnp.sum((sums[0] + sums[1]) + (sums[2] + sums[3]), axis=1, keepdims=True)
        col = col + jnp.sum(e, axis=1, keepdims=True)
        return jnp.where(lane == g, col, packed)

    packed = lax.fori_loop(0, groups, excess, jnp.zeros((8, 128), jnp.float32))
    below = jnp.where(tok_q > 0, tok_q, 1.0)
    accept = jnp.where(tok_q > 0, jnp.minimum(1.0, jnp.exp2(tok_z_ref[...] * kp - lse) / below), 0.0)
    packed = jnp.where((lane >= 32) & (lane < 64), accept, packed)
    send2[...] = packed
    recv2[me] = packed
    copies2 = share(send2, recv2, ssem2, rsem2)
    collect(send2, recv2, ssem2, rsem2)
    total = recv2[0]
    for i in range(1, n):
        total = total + recv2[i]
    stat_ref[0] = total
    inv = 1.0 / total
    for g in range(groups):
        col = jnp.sum(jnp.where(lane == g, inv, 0.0), axis=1, keepdims=True)
        norm_ref[g * 8:g * 8 + 8, :] = jnp.broadcast_to(col, (8, 128))
    for copy in copies1 + copies2:
        copy.wait_send()


def _scale_kernel(e_ref, norm_ref, stat_ref, o_ref, accept_ref, sum_ref, bonus_ref, stage, sem):
    rows, vocab = o_ref.shape
    full = vocab // 128
    slots = stage.shape[0]
    seqs = bonus_ref.shape[1]
    per = seqs // 8
    count = rows // 8

    def out_copy(g, slot):
        at = pl.ds(pl.multiple_of(g * 8, 8), 8)
        return pltpu.make_async_copy(stage.at[slot], o_ref.at[at, :], sem.at[slot])

    @pl.loop(0, count)
    def _(g):
        slot = lax.rem(g, slots)

        @pl.when(g >= slots)
        def _():
            out_copy(g - slots, slot).wait()

        at = pl.ds(pl.multiple_of(g * 8, 8), 8)
        inv = norm_ref[at, :]
        for c in range(full):
            cols = slice(c * 128, c * 128 + 128)
            stage[slot, :, cols] = e_ref[at, cols] * inv
        cols = slice(full * 128, vocab)
        stage[slot, :, cols] = e_ref[at, cols] * inv[:, :vocab - full * 128]
        out_copy(g, slot).start()

    lane = lax.broadcasted_iota(jnp.int32, (8, 128), 1)
    sub = lax.broadcasted_iota(jnp.int32, (8, 128), 0)

    def spread(packed, first):
        row = jnp.zeros((8, 128), jnp.float32)
        for g in range(per):
            col = jnp.sum(jnp.where(lane == first + g, packed, 0.0), axis=1, keepdims=True)
            row = jnp.where(lane == g * 8 + sub, col, row)
        return jnp.sum(row, axis=0, keepdims=True)[:, :seqs]

    for j in range(accept_ref.shape[0]):
        sum_ref[j:j + 1, :] = spread(stat_ref[0], j * per)
        accept_ref[j:j + 1, :] = spread(stat_ref[0], 32 + j * per)
    bonus_ref[...] = spread(stat_ref[1], count)
    for i in range(slots):
        out_copy(count - slots + i, lax.rem(count - slots + i, slots)).wait()


def solution(mesh):
    n = mesh.shape['tp']

    def local_step(hidden, norm_gain, w_head, draft_probs, draft_tokens, temperature):
        seqs, positions, width = hidden.shape
        vocab = w_head.shape[1]
        rows = seqs * positions
        draft = positions - 1
        draft_rows = seqs * draft
        q = draft_probs.transpose(1, 0, 2).reshape(draft_rows, vocab)
        vmem = pl.BlockSpec(memory_space=pltpu.VMEM)
        hbm = pl.BlockSpec(memory_space=pltpu.HBM)
        f32 = jnp.float32
        made = pl.pallas_call(
            _stream_kernel,
            out_shape=(pltpu.VMEM((draft_rows, vocab), f32),
                       pltpu.VMEM((2, 8, 128), f32),
                       pltpu.VMEM((8, 128), f32),
                       pltpu.VMEM((seqs, 128), f32),
                       pltpu.VMEM((8, 128), f32),
                       pltpu.VMEM((draft_rows, 128), jnp.int32)),
            in_specs=[hbm] * 5,
            out_specs=(vmem,) * 6,
            scratch_shapes=[
                pltpu.VMEM((seqs, positions, width), jnp.bfloat16),
                pltpu.VMEM((1, width), f32),
                pltpu.VMEM((1, seqs), f32),
                pltpu.VMEM((draft, seqs), jnp.int32),
                pltpu.VMEM((rows, width), f32),
                pltpu.VMEM((rows, width), jnp.bfloat16),
                pltpu.VMEM((draft_rows, 128), f32),
                pltpu.VMEM((DEPTH, TILE, width), jnp.bfloat16),
                pltpu.VMEM((256, width), jnp.bfloat16),
                pltpu.VMEM((rows, 128), f32),
                pltpu.VMEM((rows, 128), f32),
                pltpu.SemaphoreType.DMA((DEPTH,)),
                pltpu.SemaphoreType.DMA,
                pltpu.SemaphoreType.DMA((4,)),
            ],
            compiler_params=pltpu.CompilerParams(vmem_limit_bytes=28 * 2**20),
            name='stream',
        )(*[pltpu.with_memory_space_constraint(a, pltpu.HBM) for a in (
            hidden, norm_gain[None], temperature[None], draft_tokens.T, w_head.T)])
        z, stat, norm = pl.pallas_call(
            functools.partial(_exchange_kernel, n),
            out_shape=(pltpu.VMEM((draft_rows, vocab), f32),
                       pltpu.VMEM((2, 8, 128), f32),
                       pltpu.VMEM((draft_rows, 128), f32)),
            in_specs=[vmem] * 6 + [hbm],
            out_specs=(vmem,) * 3,
            scratch_shapes=[
                pltpu.VMEM((draft_rows, 128), f32),
                pltpu.VMEM((n, 2, 8, 128), f32),
                pltpu.VMEM((8, 128), f32),
                pltpu.VMEM((n, 8, 128), f32),
                pltpu.SemaphoreType.DMA((draft_rows // 8,)),
                pltpu.SemaphoreType.DMA((n,)),
                pltpu.SemaphoreType.DMA((n,)),
                pltpu.SemaphoreType.DMA((n,)),
                pltpu.SemaphoreType.DMA((n,)),
            ],
            compiler_params=pltpu.CompilerParams(
                collective_id=0, has_side_effects=True, vmem_limit_bytes=4 * 2**20),
            name='exchange',
        )(*[pltpu.with_memory_space_constraint(a, pltpu.VMEM) for a in made],
          pltpu.with_memory_space_constraint(q, pltpu.HBM))
        slots = 4
        residual, accept, norm_sum, bonus = pl.pallas_call(
            _scale_kernel,
            out_shape=(jax.ShapeDtypeStruct((draft_rows, vocab), f32),
                       jax.ShapeDtypeStruct((draft, seqs), f32),
                       jax.ShapeDtypeStruct((draft, seqs), f32),
                       jax.ShapeDtypeStruct((1, seqs), f32)),
            in_specs=[vmem, vmem, vmem],
            out_specs=(hbm, vmem, vmem, vmem),
            scratch_shapes=[pltpu.VMEM((slots, 8, vocab), f32), pltpu.SemaphoreType.DMA((slots,))],
            compiler_params=pltpu.CompilerParams(vmem_limit_bytes=8 * 2**20),
            name='scale',
        )(*[pltpu.with_memory_space_constraint(a, pltpu.VMEM) for a in (z, norm, stat)])
        residual = residual.reshape(draft, seqs, vocab).transpose(1, 0, 2)
        return accept.T, norm_sum.T, residual, bonus[0]

    return jax.shard_map(
        local_step,
        mesh=mesh,
        in_specs=(P('dp', None, None), P(), P(None, 'tp'), P('dp', None, 'tp'), P('dp', None), P('dp')),
        out_specs=(P('dp', None), P('dp', None), P('dp', None, 'tp'), P('dp')),
        check_vma=False,
    )
```

time: 128 us -> 62.7 us (0.49)
  Pallas kernels: 0 us -> 49.9 us
  blocking collectives: 45.8 us -> 0 us
  other arithmetic: 42 us -> 0 us
  matrix products: 30.6 us -> 0 us
  local copies, waits for them, and re-layouts: 8.67 us -> 11.9 us
    pallas_call x0 -> x3, Pallas kernels: none -> 49.9 us  [the longest x1 25.2 us: local_step(): pl.pallas_call(_stream_kernel, out_shape=(pltpu.VMEM((draft_rows, vocab),...]
    dot_general x1 -> x0, matrix products: 30.6 us -> none  [local_step(): jnp.einsum('cle,ew->clw', normed, w_head, preferred_element_type=jnp.floa...]
    psum x2 -> x0, blocking collectives: 27.5 us -> none  [local_step(): lax.psum((local_sum, tok_scaled, tok_draft), 'tp')]
    reduce_sum x3 -> x0, other arithmetic: 24.7 us -> none  [the longest x1 14.9 us: local_step(): norm_sum = lax.psum(jnp.sum(excess, axis=-1), 'tp')]
    pmax x1 -> x0, blocking collectives: 18.3 us -> none  [local_step(): row_max = lax.pmax(jnp.max(scaled, axis=-1), 'tp')]
    div x1 -> x0, other arithmetic: 15.4 us -> none  [local_step(): residual = excess / norm_sum[:, :, None]]
    unnamed x10 -> x4, local copies, waits for them, and re-layouts: 0.03 us -> 10.6 us
    gather x8 -> x0, local copies, waits for them, and re-layouts: 8.11 us -> none  [the longest x5 4.16 us: local_step(): jnp.take_along_axis(scaled[:, :draft_len], safe_idx, axis=-1)[:, :, 0]]
where the time goes in v2:
time: 62.7 us; the launch traced here: 62.4 us
  Pallas kernels  49.9 us (80%)
  local copies, waits for them, and re-layouts  11.9 us (19%)
  between operations  0.66 us (1%)
    pallas_call x1, Pallas kernels, local_step(): pl.pallas_call(_stream_kernel, out_shape=(pltpu.VMEM((draft_rows, vocab),...  25.2 us
    pallas_call x1, Pallas kernels, local_step(): pl.pallas_call(functools.partial(_exchange_kernel, n), out_shape=(pltpu.V...  18.3 us
    unnamed x4, local copies, waits for them, and re-layouts  10.6 us
    pallas_call x1, Pallas kernels, local_step(): pl.pallas_call(_scale_kernel, out_shape=(jax.ShapeDtypeStruct((draft_rows...  6.39 us
    broadcast_in_dim x1, local copies, waits for them, and re-layouts, local_step(): norm_gain[None]  1.29 us

profile of v2, /device:TPU:0, one launch (start us, length us, event | category | flops | bytes accessed | tf_op | source)
XLA Modules:
  0.0 62.4 jit_solution(7710464386551530428)
XLA Ops:
  0.6 1.3 %broadcast_in_dim.6.gain_ref = f32[1,1536]{1,0:T(1,128)} reshape(f32[1536]{0:T(1024)} %param.7) | data formatting | bytes 12288 | tf_op jit(solution)/shard_map/broadcast_in_dim | solution.py:412
  1.9 25.2 %stream.1 = (f32[192,18992]{1,0:T(8,128)S(1)}, f32[2,8,128]{2,1,0:T(8,128)S(1)}, f32[8,128]{1,0:T(8,128)S(1)}, f32[64,128]{1,0:T(8,128)S(1)}, f32[8,128]{1,0:T(8,128)S(1)}, /*index=5*/s32[192,128]{1,0:T(8,128)S(1)}) custom-call(bf16[64,4,1536]{2,1,0:T(4,128)(2,1)} %h_ref.1, f32[1,1536]{1,0:T(1,128)} %broadcast_in_dim.6.gain_ref, f32[1,64]{1,0:T(1,128)} %bitcast.15, ...), custom_call_target="tpu_custom_call" | custom-call | tf_op jit(solution)/shard_map/stream/pallas_call | solution.py:383
  27.2 18.3 %exchange.1 = (f32[192,18992]{1,0:T(8,128)S(1)}, f32[2,8,128]{2,1,0:T(8,128)S(1)}, f32[192,128]{1,0:T(8,128)S(1)}) custom-call(f32[192,18992]{1,0:T(8,128)S(1)} %get-tuple-element.17.z_ref, f32[2,8,128]{2,1,0:T(8,128)S(1)} %get-tuple-element.18.ml_ref, f32[8,128]{1,0:T(8,128)S(1)} %get-tuple-element.19.tok_z_ref, f32[64,128]{1,0:T(8,128)S(1)} %get-tuple-element.20.k_ref, ...), custom_call_target="tpu_custom_call" | custom-call | tf_op jit(solution)/shard_map/exchange/pallas_call | solution.py:413
  45.4 0.0 copy-start
  45.4 5.4 %copy-done = f32[192,18992]{1,0:T(8,128)} copy-done((f32[192,18992]{1,0:T(8,128)}, f32[192,18992]{1,0:T(8,128)S(1)}, u32[]{:S(2)}) %copy-start) | copy-done | bytes 14585880
  50.9 0.0 copy-start.1
  50.9 5.2 %copy-done.1 = f32[192,18992]{1,0:T(8,128)S(1)} copy-done((f32[192,18992]{1,0:T(8,128)S(1)}, f32[192,18992]{1,0:T(8,128)}, u32[]{:S(2)}) %copy-start.1) | copy-done | bytes 14585880
  56.1 6.4 %scale.1 = (f32[192,18992]{1,0:T(8,128)}, f32[3,64]{1,0:T(4,128)}, f32[3,64]{1,0:T(4,128)}, f32[1,64]{1,0:T(1,128)}) custom-call(f32[192,18992]{1,0:T(8,128)S(1)} %copy-done.1, f32[192,128]{1,0:T(8,128)S(1)} %get-tuple-element.24.norm_ref, f32[2,8,128]{2,1,0:T(8,128)S(1)} %get-tuple-element.25.stat_ref), custom_call_target="tpu_custom_call" | custom-call | tf_op jit(solution)/shard_map/scale/pallas_call | solution.py:437
Async XLA Ops:
  45.4 5.5 %copy-start = (f32[192,18992]{1,0:T(8,128)}, f32[192,18992]{1,0:T(8,128)S(1)}, u32[]{:S(2)}) copy-start(f32[192,18992]{1,0:T(8,128)S(1)} %get-tuple-element.23.e_ref) | copy-start | bytes 43757572
  50.9 5.2 %copy-start.1 = (f32[192,18992]{1,0:T(8,128)S(1)}, f32[192,18992]{1,0:T(8,128)}, u32[]{:S(2)}) copy-start(f32[192,18992]{1,0:T(8,128)} %copy-done) | copy-start | bytes 43757572

commit v3 on v2

--- a/solution.py
+++ b/solution.py
@@ -12,6 +12,7 @@
 MESH = pl.DeviceIdType.MESH
 TILE = 512
 DEPTH = 10
+EARLY = 3
 LOW = -3.0e38
 
 
@@ -21,8 +22,8 @@
 
 
 def _stream_kernel(h_ref, gain_ref, temp_ref, tok_ref, w_ref,
-                   z_ref, ml_ref, tok_z_ref, k_ref, kp_ref, hit_ref,
-                   hbuf, gbuf, tbuf, dbuf, hp_ref, x_ref, tz_ref, wbuf, wtail, m_ref, l_ref,
+                   z_ref, ml_ref, k_ref, kp_ref, hit_ref,
+                   hbuf, gbuf, tbuf, dbuf, hp_ref, x_ref, wbuf, wtail, m_ref, l_ref,
                    wsem, tsem, isem):
     me = lax.axis_index('tp')
     vocab = w_ref.shape[0]
@@ -51,12 +52,11 @@
         copy.start()
     tail_copy = pltpu.make_async_copy(w_ref.at[pl.ds(tail_at, tail), :], wtail.at[pl.ds(0, tail), :], tsem)
     tail_copy.start()
-    for i in range(DEPTH - 1):
+    for i in range(EARLY):
         w_copy(i).start()
 
     m_ref[...] = jnp.full_like(m_ref, LOW)
     l_ref[...] = jnp.zeros_like(l_ref)
-    tz_ref[...] = jnp.zeros_like(tz_ref)
     wtail[tail:, :] = jnp.zeros((wtail.shape[0] - tail, width), wtail.dtype)
 
     for copy in first_copies[1:]:
@@ -78,6 +78,8 @@
             hit_ref[at, :] = jnp.broadcast_to(column(row, g), (8, 128)).astype(jnp.int32)
     kp_ref[...] = kp
     first_copies[0].wait()
+    for i in range(EARLY, DEPTH - 1):
+        w_copy(i).start()
 
     def run(*accs):
         def acc(q, p, b):
@@ -97,17 +99,11 @@
 
         cols = lax.broadcasted_iota(jnp.int32, (seqs, 128), 1)
 
-        def update(b, parts, base):
+        def update(b, parts):
             at = slice(b * seqs, (b + 1) * seqs)
             k = k_ref[...]
             old = m_ref[at, :]
             new = old
-            if b < 3:
-                hit = hit_ref[at, :] - base
-                got = tz_ref[at, :]
-                for i, v in enumerate(parts):
-                    got = jnp.where(hit == cols + i * 128, v, got)
-                tz_ref[at, :] = got
             for v in parts:
                 new = jnp.maximum(new, v)
             total = l_ref[at, :] * jnp.exp2((old - new) * k)
@@ -124,13 +120,13 @@
                     at = pl.ds(pl.multiple_of(tile * TILE + q * 256, 256), 256)
                     z_ref[b * seqs:(b + 1) * seqs, at] = v
                 parts += [v[:, :128], v[:, 128:]]
-            update(b, parts, tile * TILE)
+            update(b, parts)
 
         def drain_tail(p, b):
             v = pltpu.matmul_pop(acc(0, p, b))
             if b < 3:
                 z_ref[b * seqs:(b + 1) * seqs, tail_at:tail_at + tail] = v[:, :tail]
-            update(b, [jnp.where(cols < tail, v[:, :128], LOW)], tail_at)
+            update(b, [jnp.where(cols < tail, v[:, :128], LOW)])
 
         def step(tile, p, last=False, first=False, refill=None):
             if not last:
@@ -167,7 +163,9 @@
             at = slice(g * 16, g * 16 + 16)
             h = hp_ref[at, :]
             inv_rms = lax.rsqrt(jnp.sum(h * h, axis=1, keepdims=True) * (1.0 / width) + 1e-5)
-            x_ref[at, :] = (h * inv_rms * gain).astype(jnp.bfloat16)
+            for c in range(width // 128):
+                cs = slice(c * 128, c * 128 + 128)
+                x_ref[at, cs] = (h[:, cs] * inv_rms * gain[c:c + 1, :]).astype(jnp.bfloat16)
 
         tail_copy.wait()
         for c in range(chunks):
@@ -198,7 +196,6 @@
 
     packed_m = jnp.zeros((8, 128), jnp.float32)
     packed_l = jnp.zeros((8, 128), jnp.float32)
-    tok_z = jnp.zeros((8, 128), jnp.float32)
     for g in range(all_groups):
         at = slice(g * 8, g * 8 + 8)
         m = m_ref[at, :]
@@ -207,15 +204,12 @@
         total = jnp.sum(l_ref[at, :] * jnp.exp2((m - top) * k), axis=1, keepdims=True)
         packed_m = _pack(packed_m, g, top)
         packed_l = _pack(packed_l, g, total)
-        if g < groups:
-            tok_z = _pack(tok_z, g, jnp.sum(tz_ref[at, :], axis=1, keepdims=True))
     ml_ref[0] = packed_m
     ml_ref[1] = packed_l
-    tok_z_ref[...] = tok_z
-
-
-def _exchange_kernel(n, z_ref, ml_ref, tok_z_ref, k_ref, kp_ref, hit_ref, q_ref, e_ref, stat_ref, norm_ref,
-                     lse_ref, recv1, send2, recv2, qsem, ssem1, rsem1, ssem2, rsem2):
+
+
+def _exchange_kernel(n, z_ref, ml_ref, k_ref, kp_ref, hit_ref, q_ref, e_ref, stat_ref, norm_ref,
+                     lse_ref, part_q, part_z, recv1, send2, recv2, qsem, ssem1, rsem1, ssem2, rsem2):
     me = lax.axis_index('tp')
     dp = lax.axis_index('dp')
     draft_rows, vocab = q_ref.shape
@@ -257,18 +251,30 @@
 
     copies1 = share(ml_ref, recv1, ssem1, rsem1)
 
-    def gather(g, packed):
+    @pl.loop(0, groups)
+    def _(g):
         q_copy(g).wait()
         at = pl.ds(pl.multiple_of(g * 8, 8), 8)
         hit = hit_ref[at, :]
-        got = [jnp.zeros((8, 128), jnp.float32) for _ in range(4)]
+        got_q = [jnp.zeros((8, 128), jnp.float32) for _ in range(2)]
+        got_z = [jnp.zeros((8, 128), jnp.float32) for _ in range(2)]
         for c in range(full):
-            got[c % 4] = jnp.where(hit - c * 128 == lane, e_ref[at, c * 128:c * 128 + 128], got[c % 4])
-        last = jnp.where(hit[:, :rest] - full * 128 == lane[:, :rest], e_ref[at, edge], 0.0)
-        col = jnp.sum((got[0] + got[1]) + (got[2] + got[3]), axis=1, keepdims=True)
-        return _pack(packed, g, col + jnp.sum(last, axis=1, keepdims=True))
-
-    tok_q = lax.fori_loop(0, groups, gather, jnp.zeros((8, 128), jnp.float32))
+            cols = slice(c * 128, c * 128 + 128)
+            here = hit - c * 128 == lane
+            got_q[c % 2] = jnp.where(here, e_ref[at, cols], got_q[c % 2])
+            got_z[c % 2] = jnp.where(here, z_ref[at, cols], got_z[c % 2])
+        here = hit[:, :rest] - full * 128 == lane[:, :rest]
+        part_q[at, :] = got_q[0] + got_q[1]
+        part_z[at, :] = got_z[0] + got_z[1]
+        part_q[at, :rest] = part_q[at, :rest] + jnp.where(here, e_ref[at, edge], 0.0)
+        part_z[at, :rest] = part_z[at, :rest] + jnp.where(here, z_ref[at, edge], 0.0)
+
+    tok_q = jnp.zeros((8, 128), jnp.float32)
+    tok_z = jnp.zeros((8, 128), jnp.float32)
+    for g in range(groups):
+        at = slice(g * 8, g * 8 + 8)
+        tok_q = _pack(tok_q, g, jnp.sum(part_q[at, :], axis=1, keepdims=True))
+        tok_z = _pack(tok_z, g, jnp.sum(part_z[at, :], axis=1, keepdims=True))
 
     collect(ml_ref, recv1, ssem1, rsem1)
     kp = kp_ref[...]
@@ -284,7 +290,7 @@
         col = jnp.sum(jnp.where(lane == g, lse, 0.0), axis=1, keepdims=True)
         lse_ref[g * 8:g * 8 + 8, :] = jnp.broadcast_to(col, (8, 128))
 
-    def excess(g, packed):
+    def excess(g):
         at = pl.ds(pl.multiple_of(g * 8, 8), 8)
         k = k_ref[pl.ds(pl.multiple_of(lax.rem(g, per) * 8, 8), 8), :]
         base = lse_ref[at, :]
@@ -296,13 +302,19 @@
             sums[c % 4] = sums[c % 4] + e
         e = jnp.maximum(jnp.exp2(z_ref[at, edge] * k[:, :rest] - base[:, :rest]) - e_ref[at, edge], 0.0)
         e_ref[at, edge] = e
-        col = jnp.sum((sums[0] + sums[1]) + (sums[2] + sums[3]), axis=1, keepdims=True)
-        col = col + jnp.sum(e, axis=1, keepdims=True)
-        return jnp.where(lane == g, col, packed)
-
-    packed = lax.fori_loop(0, groups, excess, jnp.zeros((8, 128), jnp.float32))
+        part_q[at, :] = (sums[0] + sums[1]) + (sums[2] + sums[3])
+        part_q[at, :rest] = part_q[at, :rest] + e
+
+    @pl.loop(0, groups // 2)
+    def _(i):
+        excess(2 * i)
+        excess(2 * i + 1)
+
+    packed = jnp.zeros((8, 128), jnp.float32)
+    for g in range(groups):
+        packed = _pack(packed, g, jnp.sum(part_q[g * 8:g * 8 + 8, :], axis=1, keepdims=True))
     below = jnp.where(tok_q > 0, tok_q, 1.0)
-    accept = jnp.where(tok_q > 0, jnp.minimum(1.0, jnp.exp2(tok_z_ref[...] * kp - lse) / below), 0.0)
+    accept = jnp.where(tok_q > 0, jnp.minimum(1.0, jnp.exp2(tok_z * kp - lse) / below), 0.0)
     packed = jnp.where((lane >= 32) & (lane < 64), accept, packed)
     send2[...] = packed
     recv2[me] = packed
@@ -384,20 +396,18 @@
             _stream_kernel,
             out_shape=(pltpu.VMEM((draft_rows, vocab), f32),
                        pltpu.VMEM((2, 8, 128), f32),
-                       pltpu.VMEM((8, 128), f32),
                        pltpu.VMEM((seqs, 128), f32),
                        pltpu.VMEM((8, 128), f32),
                        pltpu.VMEM((draft_rows, 128), jnp.int32)),
             in_specs=[hbm] * 5,
-            out_specs=(vmem,) * 6,
+            out_specs=(vmem,) * 5,
             scratch_shapes=[
                 pltpu.VMEM((seqs, positions, width), jnp.bfloat16),
-                pltpu.VMEM((1, width), f32),
+                pltpu.VMEM((width // 128, 128), f32),
                 pltpu.VMEM((1, seqs), f32),
                 pltpu.VMEM((draft, seqs), jnp.int32),
                 pltpu.VMEM((rows, width), f32),
                 pltpu.VMEM((rows, width), jnp.bfloat16),
-                pltpu.VMEM((draft_rows, 128), f32),
                 pltpu.VMEM((DEPTH, TILE, width), jnp.bfloat16),
                 pltpu.VMEM((256, width), jnp.bfloat16),
                 pltpu.VMEM((rows, 128), f32),
@@ -409,15 +419,17 @@
             compiler_params=pltpu.CompilerParams(vmem_limit_bytes=28 * 2**20),
             name='stream',
         )(*[pltpu.with_memory_space_constraint(a, pltpu.HBM) for a in (
-            hidden, norm_gain[None], temperature[None], draft_tokens.T, w_head.T)])
+            hidden, norm_gain.reshape(width // 128, 128), temperature[None], draft_tokens.T, w_head.T)])
         z, stat, norm = pl.pallas_call(
             functools.partial(_exchange_kernel, n),
             out_shape=(pltpu.VMEM((draft_rows, vocab), f32),
                        pltpu.VMEM((2, 8, 128), f32),
                        pltpu.VMEM((draft_rows, 128), f32)),
-            in_specs=[vmem] * 6 + [hbm],
+            in_specs=[vmem] * 5 + [hbm],
             out_specs=(vmem,) * 3,
             scratch_shapes=[
+                pltpu.VMEM((draft_rows, 128), f32),
+                pltpu.VMEM((draft_rows, 128), f32),
                 pltpu.VMEM((draft_rows, 128), f32),
                 pltpu.VMEM((n, 2, 8, 128), f32),
                 pltpu.VMEM((8, 128), f32),
@@ -429,11 +441,11 @@
                 pltpu.SemaphoreType.DMA((n,)),
             ],
             compiler_params=pltpu.CompilerParams(
-                collective_id=0, has_side_effects=True, vmem_limit_bytes=4 * 2**20),
+                collective_id=0, has_side_effects=True, vmem_limit_bytes=8 * 2**20),
             name='exchange',
         )(*[pltpu.with_memory_space_constraint(a, pltpu.VMEM) for a in made],
           pltpu.with_memory_space_constraint(q, pltpu.HBM))
-        slots = 4
+        slots = 8
         residual, accept, norm_sum, bonus = pl.pallas_call(
             _scale_kernel,
             out_shape=(jax.ShapeDtypeStruct((draft_rows, vocab), f32),

time: 62.7 us -> 44.1 us (0.70)
  local copies, waits for them, and re-layouts: 11.9 us -> 0 us
  Pallas kernels: 49.9 us -> 43.3 us
    unnamed x4 -> x0, local copies, waits for them, and re-layouts: 10.6 us -> none
    pallas_call x1, Pallas kernels: 25.2 us -> 20.8 us  [local_step(): pl.pallas_call(_stream_kernel, out_shape=(pltpu.VMEM((draft_rows, vocab),...]
    pallas_call x1, Pallas kernels: 18.3 us -> 16.6 us  [local_step(): pl.pallas_call(functools.partial(_exchange_kernel, n), out_shape=(pltpu.V...]
    broadcast_in_dim x1 -> x0, local copies, waits for them, and re-layouts: 1.29 us -> none  [local_step(): norm_gain[None]]
where the time goes in v3:
time: 44.1 us; the launch traced here: 43.9 us
  Pallas kernels  43.3 us (98%)
  between operations  0.65 us (1%)
    pallas_call x1, Pallas kernels, local_step(): pl.pallas_call(_stream_kernel, out_shape=(pltpu.VMEM((draft_rows, vocab),...  20.8 us
    pallas_call x1, Pallas kernels, local_step(): pl.pallas_call(functools.partial(_exchange_kernel, n), out_shape=(pltpu.V...  16.6 us
    pallas_call x1, Pallas kernels, local_step(): pl.pallas_call(_scale_kernel, out_shape=(jax.ShapeDtypeStruct((draft_rows...  5.86 us

profile of v3, /device:TPU:0, one launch (start us, length us, event | category | flops | bytes accessed | tf_op | source)
XLA Modules:
  0.0 43.9 jit_solution(17869790490107847876)
XLA Ops:
  0.6 20.8 %stream.1 = (f32[192,18992]{1,0:T(8,128)S(1)}, f32[2,8,128]{2,1,0:T(8,128)S(1)}, f32[64,128]{1,0:T(8,128)S(1)}, f32[8,128]{1,0:T(8,128)S(1)}, s32[192,128]{1,0:T(8,128)S(1)}) custom-call(bf16[64,4,1536]{2,1,0:T(4,128)(2,1)} %h_ref.1, f32[12,128]{1,0:T(8,128)} %bitcast.15, f32[1,64]{1,0:T(1,128)} %bitcast.17, s32[3,64]{1,0:T(4,128)} %bitcast.16, ...), custom_call_target="tpu_custom_call" | custom-call | tf_op jit(solution)/shard_map/stream/pallas_call | solution.py:395
  21.5 16.6 %exchange.1 = (f32[192,18992]{1,0:T(8,128)S(1)}, f32[2,8,128]{2,1,0:T(8,128)S(1)}, f32[192,128]{1,0:T(8,128)S(1)}) custom-call(f32[192,18992]{1,0:T(8,128)S(1)} %get-tuple-element.16.z_ref, f32[2,8,128]{2,1,0:T(8,128)S(1)} %get-tuple-element.17.ml_ref, f32[64,128]{1,0:T(8,128)S(1)} %get-tuple-element.18.k_ref, f32[8,128]{1,0:T(8,128)S(1)} %get-tuple-element.19.kp_ref, ...), custom_call_target="tpu_custom_call" | custom-call | tf_op jit(solution)/shard_map/exchange/pallas_call | solution.py:423
  38.1 5.9 %scale.1 = (f32[192,18992]{1,0:T(8,128)}, f32[3,64]{1,0:T(4,128)}, f32[3,64]{1,0:T(4,128)}, f32[1,64]{1,0:T(1,128)}) custom-call(f32[192,18992]{1,0:T(8,128)S(1)} %get-tuple-element.21.e_ref, f32[192,128]{1,0:T(8,128)S(1)} %get-tuple-element.22.norm_ref, f32[2,8,128]{2,1,0:T(8,128)S(1)} %get-tuple-element.23.stat_ref), custom_call_target="tpu_custom_call" | custom-call | tf_op jit(solution)/shard_map/scale/pallas_call | solution.py:449

commit v4 on v3

--- a/solution.py
+++ b/solution.py
@@ -11,8 +11,8 @@
 LN2 = 0.6931471805599453
 MESH = pl.DeviceIdType.MESH
 TILE = 512
-DEPTH = 10
-EARLY = 3
+DEPTH = 8
+EARLY = 2
 LOW = -3.0e38
 
 
@@ -22,7 +22,7 @@
 
 
 def _stream_kernel(h_ref, gain_ref, temp_ref, tok_ref, w_ref,
-                   z_ref, ml_ref, k_ref, kp_ref, hit_ref,
+                   z_ref, ml_ref, k_ref, mk_ref, kp_ref, hit_ref,
                    hbuf, gbuf, tbuf, dbuf, hp_ref, x_ref, wbuf, wtail, m_ref, l_ref,
                    wsem, tsem, isem):
     me = lax.axis_index('tp')
@@ -85,11 +85,12 @@
         def acc(q, p, b):
             return accs[(q * 2 + p) * 4 + b]
 
-        def accumulate(q, p, c):
+        def accumulate(q, p, c, staged=None):
+            staged = c % 2 if staged is None else staged
             for b in range(4):
                 pltpu.matmul_acc_lhs(
                     acc(q, p, b), x_ref[b * seqs:(b + 1) * seqs, c * 256:(c + 1) * 256],
-                    load_staged_rhs=c % 2 if b == 0 else None)
+                    load_staged_rhs=staged if b == 0 else None)
 
         def push(tile, q, c):
             slot = lax.rem(tile, DEPTH)
@@ -123,7 +124,7 @@
             update(b, parts)
 
         def drain_tail(p, b):
-            v = pltpu.matmul_pop(acc(0, p, b))
+            v = pltpu.matmul_pop(acc(0, p, b)) + pltpu.matmul_pop(acc(1, p, b))
             if b < 3:
                 z_ref[b * seqs:(b + 1) * seqs, tail_at:tail_at + tail] = v[:, :tail]
             update(b, [jnp.where(cols < tail, v[:, :128], LOW)])
@@ -149,15 +150,24 @@
 
         c_of = lax.broadcasted_iota(jnp.int32, (seqs, 256), 1)
         r_of = lax.broadcasted_iota(jnp.int32, (seqs, 256), 0)
-        for c in range(chunks):
+        def reorder(c):
             flat = hbuf[:, :, c * 256:(c + 1) * 256].reshape(rows, 256)
             pltpu.matmul_push_rhs(flat, staging_register=(c // 2) % 2, mxu_index=c % 2)
             for b in range(4):
                 pick = jnp.where(c_of == r_of * 4 + b, 1.0, 0.0).astype(jnp.bfloat16)
                 pltpu.matmul_acc_lhs(acc(c % 2, (c // 2) % 2, b), pick,
                                      load_staged_rhs=(c // 2) % 2 if b == 0 else None)
+
+        def reordered(c):
             for b in range(4):
                 hp_ref[b * seqs:(b + 1) * seqs, c * 256:(c + 1) * 256] = pltpu.matmul_pop(acc(c % 2, (c // 2) % 2, b))
+
+        for c in range(chunks):
+            if c >= 4:
+                reordered(c - 4)
+            reorder(c)
+        for c in range(max(0, chunks - 4), chunks):
+            reordered(c)
         gain = gbuf[...]
         for g in range(all_groups // 2):
             at = slice(g * 16, g * 16 + 16)
@@ -168,9 +178,12 @@
                 x_ref[at, cs] = (h[:, cs] * inv_rms * gain[c:c + 1, :]).astype(jnp.bfloat16)
 
         tail_copy.wait()
-        for c in range(chunks):
-            pltpu.matmul_push_rhs(wtail[:, c * 256:(c + 1) * 256], staging_register=c % 2, mxu_index=0, transpose=True)
-            accumulate(0, 1, c)
+        half = chunks // 2
+        for i in range(half):
+            for q in range(2):
+                c = q * half + i
+                pltpu.matmul_push_rhs(wtail[:, c * 256:(c + 1) * 256], staging_register=i % 2, mxu_index=q, transpose=True)
+                accumulate(q, 1, c, i % 2)
         w_copy(0).wait()
         for q in range(2):
             push(0, q, 0)
@@ -203,13 +216,15 @@
         k = k_ref[g % per * 8:g % per * 8 + 8, :]
         total = jnp.sum(l_ref[at, :] * jnp.exp2((m - top) * k), axis=1, keepdims=True)
         packed_m = _pack(packed_m, g, top)
+        if g < groups:
+            mk_ref[at, :] = top * k
         packed_l = _pack(packed_l, g, total)
     ml_ref[0] = packed_m
     ml_ref[1] = packed_l
 
 
-def _exchange_kernel(n, z_ref, ml_ref, k_ref, kp_ref, hit_ref, q_ref, e_ref, stat_ref, norm_ref,
-                     lse_ref, part_q, part_z, recv1, send2, recv2, qsem, ssem1, rsem1, ssem2, rsem2):
+def _exchange_kernel(n, z_ref, ml_ref, k_ref, mk_ref, kp_ref, hit_ref, q_ref, e_ref, stat_ref, norm_ref,
+                     y_ref, scale_ref, part_q, part_z, recv1, send2, recv2, qsem, ssem1, rsem1, ssem2, rsem2):
     me = lax.axis_index('tp')
     dp = lax.axis_index('dp')
     draft_rows, vocab = q_ref.shape
@@ -256,13 +271,18 @@
         q_copy(g).wait()
         at = pl.ds(pl.multiple_of(g * 8, 8), 8)
         hit = hit_ref[at, :]
+        k = k_ref[pl.ds(pl.multiple_of(lax.rem(g, per) * 8, 8), 8), :]
+        mk = mk_ref[at, :]
         got_q = [jnp.zeros((8, 128), jnp.float32) for _ in range(2)]
         got_z = [jnp.zeros((8, 128), jnp.float32) for _ in range(2)]
         for c in range(full):
             cols = slice(c * 128, c * 128 + 128)
             here = hit - c * 128 == lane
+            z = z_ref[at, cols]
+            y_ref[at, cols] = jnp.exp2(z * k - mk)
             got_q[c % 2] = jnp.where(here, e_ref[at, cols], got_q[c % 2])
-            got_z[c % 2] = jnp.where(here, z_ref[at, cols], got_z[c % 2])
+            got_z[c % 2] = jnp.where(here, z, got_z[c % 2])
+        y_ref[at, edge] = jnp.exp2(z_ref[at, edge] * k[:, :rest] - mk[:, :rest])
         here = hit[:, :rest] - full * 128 == lane[:, :rest]
         part_q[at, :] = got_q[0] + got_q[1]
         part_z[at, :] = got_z[0] + got_z[1]
@@ -288,19 +308,18 @@
     stat_ref[1] = lse * LN2
     for g in range(groups):
         col = jnp.sum(jnp.where(lane == g, lse, 0.0), axis=1, keepdims=True)
-        lse_ref[g * 8:g * 8 + 8, :] = jnp.broadcast_to(col, (8, 128))
+        scale_ref[g * 8:g * 8 + 8, :] = jnp.exp2(mk_ref[g * 8:g * 8 + 8, :] - col)
 
     def excess(g):
         at = pl.ds(pl.multiple_of(g * 8, 8), 8)
-        k = k_ref[pl.ds(pl.multiple_of(lax.rem(g, per) * 8, 8), 8), :]
-        base = lse_ref[at, :]
+        base = scale_ref[at, :]
         sums = [jnp.zeros((8, 128), jnp.float32) for _ in range(4)]
         for c in range(full):
             cols = slice(c * 128, c * 128 + 128)
-            e = jnp.maximum(jnp.exp2(z_ref[at, cols] * k - base) - e_ref[at, cols], 0.0)
+            e = jnp.maximum(y_ref[at, cols] * base - e_ref[at, cols], 0.0)
             e_ref[at, cols] = e
             sums[c % 4] = sums[c % 4] + e
-        e = jnp.maximum(jnp.exp2(z_ref[at, edge] * k[:, :rest] - base[:, :rest]) - e_ref[at, edge], 0.0)
+        e = jnp.maximum(y_ref[at, edge] * base[:, :rest] - e_ref[at, edge], 0.0)
         e_ref[at, edge] = e
         part_q[at, :] = (sums[0] + sums[1]) + (sums[2] + sums[3])
         part_q[at, :rest] = part_q[at, :rest] + e
@@ -332,7 +351,7 @@
         copy.wait_send()
 
 
-def _scale_kernel(e_ref, norm_ref, stat_ref, o_ref, accept_ref, sum_ref, bonus_ref, stage, sem):
+def _scale_kernel(e_ref, norm_ref, stat_ref, o_ref, accept_ref, sum_ref, bonus_ref, stage, small, sem, ssem):
     rows, vocab = o_ref.shape
     full = vocab // 128
     slots = stage.shape[0]
@@ -344,14 +363,8 @@
         at = pl.ds(pl.multiple_of(g * 8, 8), 8)
         return pltpu.make_async_copy(stage.at[slot], o_ref.at[at, :], sem.at[slot])
 
-    @pl.loop(0, count)
-    def _(g):
+    def scale(g):
         slot = lax.rem(g, slots)
-
-        @pl.when(g >= slots)
-        def _():
-            out_copy(g - slots, slot).wait()
-
         at = pl.ds(pl.multiple_of(g * 8, 8), 8)
         inv = norm_ref[at, :]
         for c in range(full):
@@ -361,6 +374,10 @@
         stage[slot, :, cols] = e_ref[at, cols] * inv[:, :vocab - full * 128]
         out_copy(g, slot).start()
 
+    @pl.loop(0, slots)
+    def _(g):
+        scale(g)
+
     lane = lax.broadcasted_iota(jnp.int32, (8, 128), 1)
     sub = lax.broadcasted_iota(jnp.int32, (8, 128), 0)
 
@@ -371,10 +388,27 @@
             row = jnp.where(lane == g * 8 + sub, col, row)
         return jnp.sum(row, axis=0, keepdims=True)[:, :seqs]
 
-    for j in range(accept_ref.shape[0]):
-        sum_ref[j:j + 1, :] = spread(stat_ref[0], j * per)
-        accept_ref[j:j + 1, :] = spread(stat_ref[0], 32 + j * per)
-    bonus_ref[...] = spread(stat_ref[1], count)
+    draft = accept_ref.shape[0]
+    for j in range(draft):
+        small[0, j:j + 1, :] = spread(stat_ref[0], 32 + j * per)
+        small[1, j:j + 1, :] = spread(stat_ref[0], j * per)
+    small[2, 0:1, :] = spread(stat_ref[1], count)
+    smalls = [pltpu.make_async_copy(small.at[0, pl.ds(0, draft), :], accept_ref, ssem.at[0]),
+              pltpu.make_async_copy(small.at[1, pl.ds(0, draft), :], sum_ref, ssem.at[1]),
+              pltpu.make_async_copy(small.at[2, pl.ds(0, 1), :], bonus_ref, ssem.at[2])]
+
+    @pl.loop(slots, count)
+    def _(g):
+        out_copy(g - slots, lax.rem(g, slots)).wait()
+        scale(g)
+
+        @pl.when(g == slots)
+        def _():
+            for copy in smalls:
+                copy.start()
+
+    for copy in smalls:
+        copy.wait()
     for i in range(slots):
         out_copy(count - slots + i, lax.rem(count - slots + i, slots)).wait()
 
@@ -397,10 +431,11 @@
             out_shape=(pltpu.VMEM((draft_rows, vocab), f32),
                        pltpu.VMEM((2, 8, 128), f32),
                        pltpu.VMEM((seqs, 128), f32),
+                       pltpu.VMEM((draft_rows, 128), f32),
                        pltpu.VMEM((8, 128), f32),
                        pltpu.VMEM((draft_rows, 128), jnp.int32)),
             in_specs=[hbm] * 5,
-            out_specs=(vmem,) * 5,
+            out_specs=(vmem,) * 6,
             scratch_shapes=[
                 pltpu.VMEM((seqs, positions, width), jnp.bfloat16),
                 pltpu.VMEM((width // 128, 128), f32),
@@ -425,9 +460,10 @@
             out_shape=(pltpu.VMEM((draft_rows, vocab), f32),
                        pltpu.VMEM((2, 8, 128), f32),
                        pltpu.VMEM((draft_rows, 128), f32)),
-            in_specs=[vmem] * 5 + [hbm],
+            in_specs=[vmem] * 6 + [hbm],
             out_specs=(vmem,) * 3,
             scratch_shapes=[
+                pltpu.VMEM((draft_rows, vocab), f32),
                 pltpu.VMEM((draft_rows, 128), f32),
                 pltpu.VMEM((draft_rows, 128), f32),
                 pltpu.VMEM((draft_rows, 128), f32),
@@ -441,7 +477,7 @@
                 pltpu.SemaphoreType.DMA((n,)),
             ],
             compiler_params=pltpu.CompilerParams(
-                collective_id=0, has_side_effects=True, vmem_limit_bytes=8 * 2**20),
+                collective_id=0, has_side_effects=True, vmem_limit_bytes=16 * 2**20),
             name='exchange',
         )(*[pltpu.with_memory_space_constraint(a, pltpu.VMEM) for a in made],
           pltpu.with_memory_space_constraint(q, pltpu.HBM))
@@ -453,8 +489,9 @@
                        jax.ShapeDtypeStruct((draft, seqs), f32),
                        jax.ShapeDtypeStruct((1, seqs), f32)),
             in_specs=[vmem, vmem, vmem],
-            out_specs=(hbm, vmem, vmem, vmem),
-            scratch_shapes=[pltpu.VMEM((slots, 8, vocab), f32), pltpu.SemaphoreType.DMA((slots,))],
+            out_specs=(hbm,) * 4,
+            scratch_shapes=[pltpu.VMEM((slots, 8, vocab), f32), pltpu.VMEM((3, 4, seqs), f32),
+                            pltpu.SemaphoreType.DMA((slots,)), pltpu.SemaphoreType.DMA((3,))],
             compiler_params=pltpu.CompilerParams(vmem_limit_bytes=8 * 2**20),
             name='scale',
         )(*[pltpu.with_memory_space_constraint(a, pltpu.VMEM) for a in (z, norm, stat)])

time: 44.1 us -> 42 us (0.952)
  Pallas kernels: 43.3 us -> 41.2 us
    pallas_call x1, Pallas kernels: 16.6 us -> 15.8 us  [local_step(): pl.pallas_call(functools.partial(_exchange_kernel, n), out_shape=(pltpu.V...]
    pallas_call x1, Pallas kernels: 20.8 us -> 20.1 us  [local_step(): pl.pallas_call(_stream_kernel, out_shape=(pltpu.VMEM((draft_rows, vocab),...]
    pallas_call x1, Pallas kernels: 5.86 us -> 5.31 us  [local_step(): pl.pallas_call(_scale_kernel, out_shape=(jax.ShapeDtypeStruct((draft_rows...]
where the time goes in v4:
time: 42 us; the launch traced here: 41.8 us
  Pallas kernels  41.2 us (98%)
  between operations  0.65 us (2%)
    pallas_call x1, Pallas kernels, local_step(): pl.pallas_call(_stream_kernel, out_shape=(pltpu.VMEM((draft_rows, vocab),...  20.1 us
    pallas_call x1, Pallas kernels, local_step(): pl.pallas_call(functools.partial(_exchange_kernel, n), out_shape=(pltpu.V...  15.8 us
    pallas_call x1, Pallas kernels, local_step(): pl.pallas_call(_scale_kernel, out_shape=(jax.ShapeDtypeStruct((draft_rows...  5.31 us

profile of v4, /device:TPU:0, one launch (start us, length us, event | category | flops | bytes accessed | tf_op | source)
XLA Modules:
  0.0 41.8 jit_solution(719024051092831886)
XLA Ops:
  0.6 20.1 %stream.1 = (f32[192,18992]{1,0:T(8,128)S(1)}, f32[2,8,128]{2,1,0:T(8,128)S(1)}, f32[64,128]{1,0:T(8,128)S(1)}, f32[192,128]{1,0:T(8,128)S(1)}, f32[8,128]{1,0:T(8,128)S(1)}, /*index=5*/s32[192,128]{1,0:T(8,128)S(1)}) custom-call(bf16[64,4,1536]{2,1,0:T(4,128)(2,1)} %h_ref.1, f32[12,128]{1,0:T(8,128)} %bitcast.15, f32[1,64]{1,0:T(1,128)} %bitcast.17, ...), custom_call_target="tpu_custom_call" | custom-call | tf_op jit(solution)/shard_map/stream/pallas_call | solution.py:429
  20.7 15.8 %exchange.1 = (f32[192,18992]{1,0:T(8,128)S(1)}, f32[2,8,128]{2,1,0:T(8,128)S(1)}, f32[192,128]{1,0:T(8,128)S(1)}) custom-call(f32[192,18992]{1,0:T(8,128)S(1)} %get-tuple-element.17.z_ref, f32[2,8,128]{2,1,0:T(8,128)S(1)} %get-tuple-element.18.ml_ref, f32[64,128]{1,0:T(8,128)S(1)} %get-tuple-element.19.k_ref, f32[192,128]{1,0:T(8,128)S(1)} %get-tuple-element.20.mk_ref, ...), custom_call_target="tpu_custom_call" | custom-call | tf_op jit(solution)/shard_map/exchange/pallas_call | solution.py:458
  36.5 5.3 %scale.1 = (f32[192,18992]{1,0:T(8,128)}, f32[3,64]{1,0:T(4,128)}, f32[3,64]{1,0:T(4,128)}, f32[1,64]{1,0:T(1,128)}) custom-call(f32[192,18992]{1,0:T(8,128)S(1)} %get-tuple-element.23.e_ref, f32[192,128]{1,0:T(8,128)S(1)} %get-tuple-element.24.norm_ref, f32[2,8,128]{2,1,0:T(8,128)S(1)} %get-tuple-element.25.stat_ref), custom_call_target="tpu_custom_call" | custom-call | tf_op jit(solution)/shard_map/scale/pallas_call | solution.py:485

commit v5 on v4

--- a/solution.py
+++ b/solution.py
@@ -13,6 +13,7 @@
 TILE = 512
 DEPTH = 8
 EARLY = 2
+BLOCK = 32
 LOW = -3.0e38
 
 
@@ -223,7 +224,7 @@
     ml_ref[1] = packed_l
 
 
-def _exchange_kernel(n, z_ref, ml_ref, k_ref, mk_ref, kp_ref, hit_ref, q_ref, e_ref, stat_ref, norm_ref,
+def _exchange_kernel(n, z_ref, ml_ref, k_ref, mk_ref, kp_ref, hit_ref, q_ref, e_ref, stat_ref,
                      y_ref, scale_ref, part_q, part_z, recv1, send2, recv2, qsem, ssem1, rsem1, ssem2, rsem2):
     me = lax.axis_index('tp')
     dp = lax.axis_index('dp')
@@ -310,24 +311,20 @@
         col = jnp.sum(jnp.where(lane == g, lse, 0.0), axis=1, keepdims=True)
         scale_ref[g * 8:g * 8 + 8, :] = jnp.exp2(mk_ref[g * 8:g * 8 + 8, :] - col)
 
-    def excess(g):
-        at = pl.ds(pl.multiple_of(g * 8, 8), 8)
+    @pl.loop(0, draft_rows // BLOCK)
+    def _(i):
+        at = pl.ds(pl.multiple_of(i * BLOCK, BLOCK), BLOCK)
         base = scale_ref[at, :]
-        sums = [jnp.zeros((8, 128), jnp.float32) for _ in range(4)]
+        sums = [jnp.zeros((BLOCK, 128), jnp.float32) for _ in range(2)]
         for c in range(full):
             cols = slice(c * 128, c * 128 + 128)
             e = jnp.maximum(y_ref[at, cols] * base - e_ref[at, cols], 0.0)
             e_ref[at, cols] = e
-            sums[c % 4] = sums[c % 4] + e
+            sums[c % 2] = sums[c % 2] + e
         e = jnp.maximum(y_ref[at, edge] * base[:, :rest] - e_ref[at, edge], 0.0)
         e_ref[at, edge] = e
-        part_q[at, :] = (sums[0] + sums[1]) + (sums[2] + sums[3])
+        part_q[at, :] = sums[0] + sums[1]
         part_q[at, :rest] = part_q[at, :rest] + e
-
-    @pl.loop(0, groups // 2)
-    def _(i):
-        excess(2 * i)
-        excess(2 * i + 1)
 
     packed = jnp.zeros((8, 128), jnp.float32)
     for g in range(groups):
@@ -343,15 +340,11 @@
     for i in range(1, n):
         total = total + recv2[i]
     stat_ref[0] = total
-    inv = 1.0 / total
-    for g in range(groups):
-        col = jnp.sum(jnp.where(lane == g, inv, 0.0), axis=1, keepdims=True)
-        norm_ref[g * 8:g * 8 + 8, :] = jnp.broadcast_to(col, (8, 128))
     for copy in copies1 + copies2:
         copy.wait_send()
 
 
-def _scale_kernel(e_ref, norm_ref, stat_ref, o_ref, accept_ref, sum_ref, bonus_ref, stage, small, sem, ssem):
+def _scale_kernel(e_ref, stat_ref, o_ref, accept_ref, sum_ref, bonus_ref, stage, small, sem, ssem):
     rows, vocab = o_ref.shape
     full = vocab // 128
     slots = stage.shape[0]
@@ -363,10 +356,14 @@
         at = pl.ds(pl.multiple_of(g * 8, 8), 8)
         return pltpu.make_async_copy(stage.at[slot], o_ref.at[at, :], sem.at[slot])
 
+    lane = lax.broadcasted_iota(jnp.int32, (8, 128), 1)
+    sub = lax.broadcasted_iota(jnp.int32, (8, 128), 0)
+    inverse = 1.0 / stat_ref[0]
+
     def scale(g):
         slot = lax.rem(g, slots)
         at = pl.ds(pl.multiple_of(g * 8, 8), 8)
-        inv = norm_ref[at, :]
+        inv = jnp.broadcast_to(jnp.sum(jnp.where(lane == g, inverse, 0.0), axis=1, keepdims=True), (8, 128))
         for c in range(full):
             cols = slice(c * 128, c * 128 + 128)
             stage[slot, :, cols] = e_ref[at, cols] * inv
@@ -377,9 +374,6 @@
     @pl.loop(0, slots)
     def _(g):
         scale(g)
-
-    lane = lax.broadcasted_iota(jnp.int32, (8, 128), 1)
-    sub = lax.broadcasted_iota(jnp.int32, (8, 128), 0)
 
     def spread(packed, first):
         row = jnp.zeros((8, 128), jnp.float32)
@@ -455,13 +449,12 @@
             name='stream',
         )(*[pltpu.with_memory_space_constraint(a, pltpu.HBM) for a in (
             hidden, norm_gain.reshape(width // 128, 128), temperature[None], draft_tokens.T, w_head.T)])
-        z, stat, norm = pl.pallas_call(
+        z, stat = pl.pallas_call(
             functools.partial(_exchange_kernel, n),
             out_shape=(pltpu.VMEM((draft_rows, vocab), f32),
-                       pltpu.VMEM((2, 8, 128), f32),
-                       pltpu.VMEM((draft_rows, 128), f32)),
+                       pltpu.VMEM((2, 8, 128), f32)),
             in_specs=[vmem] * 6 + [hbm],
-            out_specs=(vmem,) * 3,
+            out_specs=(vmem,) * 2,
             scratch_shapes=[
                 pltpu.VMEM((draft_rows, vocab), f32),
                 pltpu.VMEM((draft_rows, 128), f32),
@@ -488,13 +481,13 @@
                        jax.ShapeDtypeStruct((draft, seqs), f32),
                        jax.ShapeDtypeStruct((draft, seqs), f32),
                        jax.ShapeDtypeStruct((1, seqs), f32)),
-            in_specs=[vmem, vmem, vmem],
+            in_specs=[vmem, vmem],
             out_specs=(hbm,) * 4,
             scratch_shapes=[pltpu.VMEM((slots, 8, vocab), f32), pltpu.VMEM((3, 4, seqs), f32),
                             pltpu.SemaphoreType.DMA((slots,)), pltpu.SemaphoreType.DMA((3,))],
             compiler_params=pltpu.CompilerParams(vmem_limit_bytes=8 * 2**20),
             name='scale',
-        )(*[pltpu.with_memory_space_constraint(a, pltpu.VMEM) for a in (z, norm, stat)])
+        )(*[pltpu.with_memory_space_constraint(a, pltpu.VMEM) for a in (z, stat)])
         residual = residual.reshape(draft, seqs, vocab).transpose(1, 0, 2)
         return accept.T, norm_sum.T, residual, bonus[0]
 

time: 42 us -> 41.8 us (level)
  no operation moved by 1% of the time
where the time goes in v5:
time: 41.8 us; the launch traced here: 41.6 us
  Pallas kernels  41 us (98%)
  between operations  0.65 us (2%)
    pallas_call x1, Pallas kernels, local_step(): pl.pallas_call(_stream_kernel, out_shape=(pltpu.VMEM((draft_rows, vocab),...  20.1 us
    pallas_call x1, Pallas kernels, local_step(): pl.pallas_call(functools.partial(_exchange_kernel, n), out_shape=(pltpu.V...  15.5 us
    pallas_call x1, Pallas kernels, local_step(): pl.pallas_call(_scale_kernel, out_shape=(jax.ShapeDtypeStruct((draft_rows...  5.39 us

profile of v5, /device:TPU:0, one launch (start us, length us, event | category | flops | bytes accessed | tf_op | source)
XLA Modules:
  0.0 41.6 jit_solution(14017382834601081896)
XLA Ops:
  0.6 20.1 %stream.1 = (f32[192,18992]{1,0:T(8,128)S(1)}, f32[2,8,128]{2,1,0:T(8,128)S(1)}, f32[64,128]{1,0:T(8,128)S(1)}, f32[192,128]{1,0:T(8,128)S(1)}, f32[8,128]{1,0:T(8,128)S(1)}, /*index=5*/s32[192,128]{1,0:T(8,128)S(1)}) custom-call(bf16[64,4,1536]{2,1,0:T(4,128)(2,1)} %h_ref.1, f32[12,128]{1,0:T(8,128)} %bitcast.15, f32[1,64]{1,0:T(1,128)} %bitcast.17, ...), custom_call_target="tpu_custom_call" | custom-call | tf_op jit(solution)/shard_map/stream/pallas_call | solution.py:423
  20.7 15.5 %exchange.1 = (f32[192,18992]{1,0:T(8,128)S(1)}, f32[2,8,128]{2,1,0:T(8,128)S(1)}) custom-call(f32[192,18992]{1,0:T(8,128)S(1)} %get-tuple-element.16.z_ref, f32[2,8,128]{2,1,0:T(8,128)S(1)} %get-tuple-element.17.ml_ref, f32[64,128]{1,0:T(8,128)S(1)} %get-tuple-element.18.k_ref, f32[192,128]{1,0:T(8,128)S(1)} %get-tuple-element.19.mk_ref, ...), custom_call_target="tpu_custom_call" | custom-call | tf_op jit(solution)/shard_map/exchange/pallas_call | solution.py:452
  36.3 5.4 %scale.1 = (f32[192,18992]{1,0:T(8,128)}, f32[3,64]{1,0:T(4,128)}, f32[3,64]{1,0:T(4,128)}, f32[1,64]{1,0:T(1,128)}) custom-call(f32[192,18992]{1,0:T(8,128)S(1)} %get-tuple-element.22.e_ref, f32[2,8,128]{2,1,0:T(8,128)S(1)} %get-tuple-element.23.stat_ref), custom_call_target="tpu_custom_call" | custom-call | tf_op jit(solution)/shard_map/scale/pallas_call | solution.py:478
